TPU v7x, 32 devices: a whole 2x2x4 slice. The times are simulated.
32 devices in a mesh: gx: 4 (over z), gy: 4 (over y, x), gz: 2 (over core).
Axes of the slice: x: 2, y: 2, z: 4, core: 2. Of those that a mesh axis runs over, the one named last changes fastest.
Arguments:
- cell_index: int32 [4, 4, 2, 8192], P('gx', 'gy', 'gz'), may hold values from 1431 to 167568, as said below
- offsets: float32 [4, 4, 2, 3, 8192], P('gx', 'gy', 'gz'), may hold values from -0.5 to 0.5
- mass: float32 [4, 4, 2, 8192], P('gx', 'gy', 'gz'), may hold values from 0.5 to 2
- counts: int32 [4, 4, 2], P('gx', 'gy', 'gz'), may hold values from 2048 to 8192, as said below
Outputs:
- density: float32 [512, 4, 8, 256], P(None, 'gx', 'gy', 'gz')
- spectrum: float32 [2, 256, 4, 8, 256], P(None, None, 'gx', 'gy', 'gz')
Inputs may be any that keep to these rules, and one draw needn't show every extreme that they name: `cell_index`: each entry is (i + 1) * 10 * 130 + (j + 1) * 130 + k + 1 for a cell (i, j, k) with 0 <= i < 128, 0 <= j < 8, 0 <= k < 128; slots past a block's count hold such indices too. `counts`: some block is full in every draw.
All inputs are finite; a program needn't handle non-finite values.
Results may differ from a plain program's by a relative error of at most 0.0003.
Values sent between devices are 32-bit elements; how exact they have to be, the bound alone decides.
A program may use at most 64 MiB of HBM per device.

v0:
```python
import functools
import math

import jax
import jax.numpy as jnp
import numpy as np
from jax import lax
from jax.experimental import pallas as pl
from jax.experimental.pallas import tpu as pltpu
from jax.sharding import PartitionSpec as P

MESH = pl.DeviceIdType.MESH
CX = 128
YP = 2
CZ = 128


def up(n, m):
    return -(-n // m) * m


def split(value):
    high = value.astype(jnp.bfloat16)
    low = (value - high.astype(jnp.float32)).astype(jnp.bfloat16)
    return high, low


def nt_dot(lhs, rhs):
    return lax.dot_general(lhs, rhs, (((1,), (1,)), ((), ())), preferred_element_type=jnp.float32)


def gather(full, rows):
    return (full[:rows, :128] + full[rows:, :128]) + (full[:rows, 128:] + full[rows:, 128:])


BODY = YP * CX
ROWS = BODY + 8


def paint_kernel(dims, chunk, live_ref, cell_ref, off_ref, mass_ref, out_ref, near, far, base, step_y, zrhs, lhs, accx, accz, corner, fold_x, fold_z, zin, yout, yin, pen, inbox, z_send, z_recv, y_send, y_recv, x_send, x_recv):
    groups, count_y, count_z = dims
    padded_y = YP * groups + 2
    band = up(padded_y, 8)
    stride_y = CZ + 2
    stride_x = padded_y * stride_y
    total = cell_ref.shape[1]
    pieces = total // chunk
    gx, gy, gz = lax.axis_index("gx"), lax.axis_index("gy"), lax.axis_index("gz")
    y_next = (lax.rem(gy + count_y - 1, count_y), lax.rem(gy + 1, count_y))
    z_next = (lax.rem(gz + count_z - 1, count_z), lax.rem(gz + 1, count_z))
    barrier = pltpu.get_barrier_semaphore()
    for other in z_next:
        pl.semaphore_signal(barrier, inc=1, device_id={"gz": other}, device_id_type=MESH)
    for other in y_next:
        pl.semaphore_signal(barrier, inc=1, device_id={"gy": other}, device_id_type=MESH)
    for step in range(1, groups):
        pl.semaphore_signal(barrier, inc=1, device_id={"gx": lax.rem(gx + step, groups)}, device_id_type=MESH)

    live = live_ref[0]
    accx[...] = jnp.zeros_like(accx)
    accz[...] = jnp.zeros_like(accz)
    corner[...] = jnp.zeros_like(corner)
    row_core = lax.broadcasted_iota(jnp.int32, (CX, chunk), 0).astype(jnp.float32) + 1.0
    row_band = lax.broadcasted_iota(jnp.int32, (2 * band, chunk), 0).astype(jnp.float32)

    def prepare(turn, carry):
        start = pl.multiple_of(turn * chunk, chunk)
        here = pl.ds(start, chunk)
        slot = start + lax.broadcasted_iota(jnp.int32, (1, chunk), 1)
        loaded = jnp.where(slot < live, mass_ref[:, here], 0.0)
        cell = cell_ref[:, here].astype(jnp.float32)
        x0 = jnp.floor((cell + 0.5) * (1.0 / stride_x))
        rest = cell - x0 * stride_x
        y0 = jnp.floor((rest + 0.5) * (1.0 / stride_y))
        z0 = rest - y0 * stride_y
        dx, dy, dz = off_ref[0, :, here], off_ref[1, :, here], off_ref[2, :, here]
        x1 = x0 + jnp.where(dx >= 0.0, 1.0, -1.0)
        y1 = y0 + jnp.where(dy >= 0.0, 1.0, -1.0)
        z1 = z0 + jnp.where(dz >= 0.0, 1.0, -1.0)
        fx, fy, fz = jnp.abs(dx), jnp.abs(dy), jnp.abs(dz)
        ex, ey, ez = 1.0 - fx, 1.0 - fy, 1.0 - fz
        my0, my1 = ey * loaded, fy * loaded
        base[:, here] = y0
        step_y[:, here] = y1
        zhot = jnp.where(row_core == z0, ez, jnp.where(row_core == z1, fz, 0.0))
        zhi, zlo = split(zhot)
        zboth = jnp.concatenate([zhi, zlo], axis=0)
        zrhs[turn] = zboth
        xhot = jnp.where(row_core == x0, ex, jnp.where(row_core == x1, fx, 0.0))
        xhi, xlo = split(xhot)
        near[turn] = xhot * my0
        far[turn] = xhot * my1
        yhot = jnp.where(row_band == y0, my0, jnp.where(row_band == y1, my1, 0.0)) + jnp.where(
            row_band == y0 + band, my0, jnp.where(row_band == y1 + band, my1, 0.0)
        )
        side = jnp.where(row_band >= band, 1.0, 0.0)
        ghost_x = jnp.where(x1 == side * (CX + 1.0), fx, 0.0) * yhot
        ghost_z = jnp.where(z1 == side * (CZ + 1.0), fz, 0.0) * yhot
        accx[...] += nt_dot(jnp.concatenate(split(ghost_x), axis=0), zboth)
        accz[...] += nt_dot(jnp.concatenate(split(ghost_z), axis=0), jnp.concatenate([xhi, xlo], axis=0))
        for which, edge in enumerate((0.0, CX + 1.0)):
            part = ghost_z * jnp.where(x1 == edge, fx, 0.0)
            for piece in range(chunk // 128):
                corner[which] += part[:, piece * 128 : (piece + 1) * 128]
        return carry

    lax.fori_loop(0, pieces, prepare, 0)
    fold_z[:, :CX] = gather(accz[...], 2 * band)
    lane_band = lax.broadcasted_iota(jnp.int32, (2 * band, 128), 1)
    low = jnp.sum(corner[0], axis=1, keepdims=True)
    high = jnp.sum(corner[1], axis=1, keepdims=True)
    fold_z[:, CX:] = jnp.where(lane_band == 0, low, jnp.where(lane_band == 1, high, 0.0))
    edge = gather(accx[...], 2 * band)
    pl.semaphore_wait(barrier, groups + 3)
    z_copies = [
        pltpu.make_async_remote_copy(
            src_ref=fold_z.at[pl.ds(side * band, band)],
            dst_ref=zin.at[side],
            send_sem=z_send.at[side],
            recv_sem=z_recv.at[side],
            device_id={"gz": z_next[side]},
            device_id_type=MESH,
        )
        for side in range(2)
    ]
    for copy in z_copies:
        copy.start()

    def paint_rows(first, second):
        sums = None
        for piece in range(pieces):
            here = pl.ds(piece * chunk, chunk)
            y0, y1 = base[:, here], step_y[:, here]
            for index, y in enumerate((first, second)):
                value = jnp.where(y0 == y, near[piece], jnp.where(y1 == y, far[piece], 0.0))
                high, low = split(value)
                lhs[piece, pl.ds(index * 2 * CX, CX)] = high
                lhs[piece, pl.ds(index * 2 * CX + CX, CX)] = low
            part = nt_dot(lhs[piece], zrhs[piece])
            sums = part if sums is None else sums + part
        return gather(sums[: 2 * CX], CX), gather(sums[2 * CX :], CX)

    lane = lax.broadcasted_iota(jnp.int32, (CX, CZ), 1)
    band_row = lax.broadcasted_iota(jnp.int32, (2 * CX, band), 1)

    def fold(target, rows, indices):
        for place, (whole, index) in enumerate(zip(rows, indices)):
            for side, spot in enumerate((CZ - 1, 0)):
                column = jnp.sum(jnp.where(band_row == index, columns[side], 0.0), axis=1, keepdims=True)
                whole = whole + jnp.where(lane == spot, column[:CX], 0.0)
            target[pl.ds(place * CX, CX)] = whole
            for side in range(2):
                target[pl.ds(BODY + 2 * side + place, 1)] = fold_x[side, pl.ds(index, 1)]

    def pencil_of(turn):
        half = groups // 2
        upper = gx // half
        mine = upper * (groups - 1) + (1 - 2 * upper) * gx
        near_by = turn - (groups - half)
        near_by = near_by + jnp.where(near_by >= mine, 1, 0)
        spot = jnp.where(turn < groups - half, half + turn, jnp.where(turn == groups - 1, mine, near_by))
        return upper * (groups - 1) + (1 - 2 * upper) * spot

    def pencil_copy(target):
        return pltpu.make_async_remote_copy(
            src_ref=pen.at[target],
            dst_ref=inbox.at[gx],
            send_sem=x_send.at[target],
            recv_sem=x_recv.at[gx],
            device_id={"gx": target},
            device_id_type=MESH,
        )

    def pencil_rows(turn):
        target = pencil_of(turn)
        first = 1 + target * YP
        return target, [first + row for row in range(YP)]

    def as_float(indices):
        return [jnp.asarray(index, jnp.int32).astype(jnp.float32) for index in indices]

    start_target, start_indices = pencil_rows(0)
    start_rows = paint_rows(*as_float(start_indices))
    for copy in z_copies:
        copy.wait()
    columns = [zin[side].T for side in range(2)]
    edge_lane = lax.broadcasted_iota(jnp.int32, (band, CZ), 1)
    for x_side in range(2):
        part = edge[x_side * band : (x_side + 1) * band]
        part = part + jnp.where(edge_lane == CZ - 1, zin[0][:, CX + x_side : CX + x_side + 1], 0.0)
        fold_x[x_side] = part + jnp.where(edge_lane == 0, zin[1][:, CX + x_side : CX + x_side + 1], 0.0)
    for ref in [pen.at[t] for t in range(groups)] + [yout.at[0]]:
        ref[pl.ds(BODY, 8)] = jnp.zeros((8, CZ), jnp.float32)
    fold(pen.at[start_target], start_rows, start_indices)
    pencil_copy(start_target).start()

    ghosts = [0, padded_y - 1]
    fold(yout.at[0], paint_rows(*as_float(ghosts)), ghosts)
    y_copies = [
        pltpu.make_async_remote_copy(
            src_ref=yout.at[0, pl.ds(side * CX, CX)],
            dst_ref=yin.at[side],
            send_sem=y_send.at[side],
            recv_sem=y_recv.at[side],
            device_id={"gy": y_next[side]},
            device_id_type=MESH,
        )
        for side in range(2)
    ] + [
        pltpu.make_async_remote_copy(
            src_ref=yout.at[0, pl.ds(BODY, 8)],
            dst_ref=yin.at[2 + side, pl.ds(0, 8)],
            send_sem=y_send.at[2 + side],
            recv_sem=y_recv.at[2 + side],
            device_id={"gy": y_next[side]},
            device_id_type=MESH,
        )
        for side in range(2)
    ]
    for copy in y_copies:
        copy.start()

    def visit(turn, carry):
        target, indices = pencil_rows(turn)
        rows = paint_rows(*as_float(indices))

        @pl.when(turn == 1)
        def _():
            for copy in y_copies:
                copy.wait()

        fold(pen.at[target], rows, indices)

        @pl.when(target == 0)
        def _():
            pen[0, pl.ds(0, CX)] += yin[1]
            for side in range(2):
                pen[0, pl.ds(BODY + 2 * side, 1)] += yin[3, pl.ds(2 * side + 1, 1)]

        @pl.when(target == groups - 1)
        def _():
            pen[groups - 1, pl.ds((YP - 1) * CX, CX)] += yin[0]
            for side in range(2):
                pen[groups - 1, pl.ds(BODY + 2 * side + YP - 1, 1)] += yin[2, pl.ds(2 * side, 1)]

        @pl.when(turn < groups - 1)
        def _():
            pencil_copy(target).start()

        return carry

    lax.fori_loop(1, groups, visit, 0)
    out_ref[gx] = pen[gx]
    for step in range(1, groups):
        source = lax.rem(gx + step, groups)
        pencil_copy(source).wait_send()
        pltpu.make_async_remote_copy(
            src_ref=pen.at[source],
            dst_ref=inbox.at[source],
            send_sem=x_send.at[source],
            recv_sem=x_recv.at[source],
            device_id={"gx": source},
            device_id_type=MESH,
        ).wait_recv()
        out_ref[source] = inbox[source]


def paint(dims, cell, offs, mass, live):
    groups = dims[0]
    total = cell.shape[1]
    chunk = math.gcd(2048, total)
    band = up(YP * groups + 2, 8)
    pieces = total // chunk
    vmem = pl.BlockSpec(memory_space=pltpu.VMEM)
    dma = pltpu.SemaphoreType.DMA
    return pl.pallas_call(
        functools.partial(paint_kernel, dims, chunk),
        out_shape=jax.ShapeDtypeStruct((groups, ROWS, CZ), jnp.float32),
        in_specs=[pl.BlockSpec(memory_space=pltpu.SMEM), vmem, vmem, vmem],
        out_specs=vmem,
        scratch_shapes=[
            pltpu.VMEM((pieces, CX, chunk), jnp.float32),
            pltpu.VMEM((pieces, CX, chunk), jnp.float32),
            pltpu.VMEM((1, total), jnp.float32),
            pltpu.VMEM((1, total), jnp.float32),
            pltpu.VMEM((pieces, 2 * CZ, chunk), jnp.bfloat16),
            pltpu.VMEM((pieces, 2 * BODY, chunk), jnp.bfloat16),
            pltpu.VMEM((4 * band, 256), jnp.float32),
            pltpu.VMEM((4 * band, 256), jnp.float32),
            pltpu.VMEM((2, 2 * band, 128), jnp.float32),
            pltpu.VMEM((2, band, CZ), jnp.float32),
            pltpu.VMEM((2 * band, 2 * CX), jnp.float32),
            pltpu.VMEM((2, band, 2 * CX), jnp.float32),
            pltpu.VMEM((1, ROWS, CZ), jnp.float32),
            pltpu.VMEM((4, CX, CZ), jnp.float32),
            pltpu.VMEM((groups, ROWS, CZ), jnp.float32),
            pltpu.VMEM((groups, ROWS, CZ), jnp.float32),
            dma((2,)),
            dma((2,)),
            dma((4,)),
            dma((4,)),
            dma((groups,)),
            dma((groups,)),
        ],
        compiler_params=pltpu.CompilerParams(collective_id=0, has_side_effects=True),
    )(live, cell, offs, mass)


def wave_kernel(groups, in_ref, fhi, flo, dens_ref, spec_ref, flat):
    length = groups * CX
    row_id = lax.broadcasted_iota(jnp.int32, (CX, CZ), 0)
    for block in range(groups):
        before, after = (block - 1) % groups, (block + 1) % groups
        for row in range(YP):
            value = in_ref[block, row * CX : (row + 1) * CX]
            upper = BODY + 2 + row
            value = value + jnp.where(row_id == 0, in_ref[before, upper : upper + 1], 0.0)
            lower = BODY + row
            value = value + jnp.where(row_id == CX - 1, in_ref[after, lower : lower + 1], 0.0)
            dens_ref[pl.ds(block * BODY + row, CX, stride=YP), :] = value
            high, low = split(value)
            flat[0, pl.ds(block * CX, CX), pl.ds(row * CZ, CZ)] = high
            flat[1, pl.ds(block * CX, CX), pl.ds(row * CZ, CZ)] = low
    tile = 256

    def transform(turn, carry):
        start = pl.multiple_of(turn * tile, tile)
        rows = pl.ds(start, tile)
        both = jnp.dot(fhi[rows, :], flat[0], preferred_element_type=jnp.float32)
        both += jnp.dot(flo[rows, :], flat[0], preferred_element_type=jnp.float32)
        both += jnp.dot(fhi[rows, :], flat[1], preferred_element_type=jnp.float32)
        for row in range(YP):
            spec_ref[pl.ds(start * YP + row, tile, stride=YP), :] = both[:, row * CZ : (row + 1) * CZ]
        return carry

    lax.fori_loop(0, length // tile, transform, 0)


def waves(groups, pencils):
    length = groups * CX
    half = length // 2
    angle = (np.arange(half)[:, None] * np.arange(length)[None, :] % length) * (2.0 * np.pi / length)
    table = np.concatenate([np.cos(angle), -np.sin(angle)]) / np.sqrt(length)
    fhi = table.astype(jnp.bfloat16)
    flo = (table - fhi.astype(np.float64)).astype(jnp.bfloat16)
    vmem = pl.BlockSpec(memory_space=pltpu.VMEM)
    return pl.pallas_call(
        functools.partial(wave_kernel, groups),
        out_shape=[
            jax.ShapeDtypeStruct((length * YP, CZ), jnp.float32),
            jax.ShapeDtypeStruct((2 * half * YP, CZ), jnp.float32),
        ],
        in_specs=[vmem] * 3,
        out_specs=[vmem] * 2,
        scratch_shapes=[pltpu.VMEM((2, length, YP * CZ), jnp.bfloat16)],
    )(pencils, jnp.asarray(fhi), jnp.asarray(flo))


def body(dims, cell_index, offsets, mass, counts):
    length = dims[0] * CX
    pencils = paint(
        dims, cell_index.reshape(1, -1), offsets.reshape(3, 1, -1), mass.reshape(1, -1), counts.reshape(1)
    )
    density, spectrum = waves(dims[0], pencils)
    return (density.reshape(length, 1, YP, CZ), spectrum.reshape(2, length // 2, 1, YP, CZ))


def solution(mesh):
    dims = tuple(mesh.shape[axis] for axis in ("gx", "gy", "gz"))
    placed = (
        P("gx", "gy", "gz", None),
        P("gx", "gy", "gz", None, None),
        P("gx", "gy", "gz", None),
        P("gx", "gy", "gz"),
    )
    return jax.shard_map(
        functools.partial(body, dims),
        mesh=mesh,
        in_specs=placed,
        out_specs=(P(None, "gx", "gy", "gz"), P(None, None, "gx", "gy", "gz")),
        check_vma=False,
    )
```

profile of v0, /device:TPU:0, one launch (start us, length us, event | category | flops | bytes accessed | tf_op | source)
XLA Modules:
  0.0 39.2 jit_solution(9708323033191835243)
XLA Ops:
  1.3 34.8 %shard_map.77.in_ref = f32[4,264,128]{2,1,0:T(8,128)} custom-call(s32[1]{0:T(128)} %bitcast.10.live_ref, s32[1,8192]{1,0:T(1,128)} %bitcast.12, f32[3,1,8192]{2,1,0:T(1,128)} %bitcast.11, f32[1,8192]{1,0:T(1,128)} %bitcast.13), custom_call_target="tpu_custom_call" | custom-call | tf_op jit(solution)/shard_map/pallas_call | solution.py:276
  36.1 3.0 %shard_map.78 = (f32[1024,128]{1,0:T(8,128)}, f32[1024,128]{1,0:T(8,128)}) custom-call(f32[4,264,128]{2,1,0:T(8,128)} %shard_map.77.in_ref, bf16[512,512]{1,0:T(8,128)(2,1)} %constant.4.clone.fhi, bf16[512,512]{1,0:T(8,128)(2,1)} %constant.5.clone.flo), custom_call_target="tpu_custom_call" | custom-call | tf_op jit(solution)/shard_map/pallas_call | solution.py:347
where the time goes:
time: 39.3 us; the launch traced here: 39.2 us
  Pallas kernels  37.9 us (96%)
  between operations  1.28 us (3%)
    pallas_call x1, Pallas kernels, paint(): pl.pallas_call(functools.partial(paint_kernel, dims, chunk), out_shape=ja...  34.8 us
    pallas_call x1, Pallas kernels, waves(): pl.pallas_call(functools.partial(wave_kernel, groups), out_shape=[jax.Sha...  3.03 us

commit v1 on v0

v1 whole, which is shorter than its diff:
```python
import functools
import math

import jax
import jax.numpy as jnp
import numpy as np
from jax import lax
from jax.experimental import pallas as pl
from jax.experimental.pallas import tpu as pltpu
from jax.sharding import PartitionSpec as P

MESH = pl.DeviceIdType.MESH
CX = 128
YP = 2
CZ = 128


def up(n, m):
    return -(-n // m) * m


def split(value):
    high = value.astype(jnp.bfloat16)
    low = (value - high.astype(jnp.float32)).astype(jnp.bfloat16)
    return high, low


def nt_dot(lhs, rhs):
    return lax.dot_general(lhs, rhs, (((1,), (1,)), ((), ())), preferred_element_type=jnp.float32)


def gather(full, rows):
    return (full[:rows, :128] + full[rows:, :128]) + (full[:rows, 128:] + full[rows:, 128:])


BODY = YP * CX
ROWS = BODY + 8


def parts(value):
    high = value.astype(jnp.bfloat16).astype(jnp.float32)
    return high, value - high


def paint_kernel(dims, live_ref, cell_ref, off_ref, mass_ref, out_ref, rows_x, rows_z, weigh, spot, zrhs, xrhs, lhs, glhs, crhs, accx, accz, accc, columns, fold_x, fold_z, zin, yout, yin, pen, inbox, z_send, z_recv, y_send, y_recv, x_send, x_recv):
    groups, count_y, count_z = dims
    padded_y = YP * groups + 2
    band = up(padded_y, 16)
    stride_y = CZ + 2
    stride_x = padded_y * stride_y
    lines = cell_ref.shape[0]
    span = min(16, lines)
    pieces = lines // span
    gx, gy, gz = lax.axis_index("gx"), lax.axis_index("gy"), lax.axis_index("gz")
    y_next = (lax.rem(gy + count_y - 1, count_y), lax.rem(gy + 1, count_y))
    z_next = (lax.rem(gz + count_z - 1, count_z), lax.rem(gz + 1, count_z))
    barrier = pltpu.get_barrier_semaphore()
    for other in z_next:
        pl.semaphore_signal(barrier, inc=1, device_id={"gz": other}, device_id_type=MESH)
    for other in y_next:
        pl.semaphore_signal(barrier, inc=1, device_id={"gy": other}, device_id_type=MESH)
    for step in range(1, groups):
        pl.semaphore_signal(barrier, inc=1, device_id={"gx": lax.rem(gx + step, groups)}, device_id_type=MESH)

    live = live_ref[0]
    slot = lax.broadcasted_iota(jnp.int32, (lines, 128), 0) * 128 + lax.broadcasted_iota(jnp.int32, (lines, 128), 1)
    loaded = jnp.where(slot < live, mass_ref[...], 0.0)
    cell = cell_ref[...].astype(jnp.float32)
    x0 = jnp.floor((cell + 0.5) * (1.0 / stride_x))
    rest = cell - x0 * stride_x
    y0 = jnp.floor((rest + 0.5) * (1.0 / stride_y))
    z0 = rest - y0 * stride_y
    dx, dy, dz = off_ref[0], off_ref[1], off_ref[2]
    x1 = x0 + jnp.where(dx >= 0.0, 1.0, -1.0)
    y1 = y0 + jnp.where(dy >= 0.0, 1.0, -1.0)
    z1 = z0 + jnp.where(dz >= 0.0, 1.0, -1.0)
    fx, fy, fz = jnp.abs(dx), jnp.abs(dy), jnp.abs(dz)
    ex, ey, ez = 1.0 - fx, 1.0 - fy, 1.0 - fz
    my0, my1 = ey * loaded, fy * loaded
    spot[0], spot[1], spot[2], spot[3] = y0, y1, my0, my1
    spot[4], spot[5] = ex, fx
    for index, value in enumerate((x0, x1) + parts(ex) + parts(fx)):
        rows_x[index] = value
    for index, value in enumerate((z0, z1) + parts(ez) + parts(fz)):
        rows_z[index] = value
    far_x, far_z = CX + 1.0, CZ + 1.0
    gx_y = jnp.where(x1 == 0.0, 0.0, jnp.where(x1 == far_x, float(band), -1.0 - band))
    gz_y = jnp.where(z1 == 0.0, 0.0, jnp.where(z1 == far_z, float(band), -1.0 - band))
    ghost_rows = (
        (gz_y + y0, gz_y + y1) + parts(fz * my0) + parts(fz * my1),
        (gx_y + y0, gx_y + y1) + parts(fx * my0) + parts(fx * my1),
    )
    for kind in range(2):
        for index, value in enumerate(ghost_rows[kind]):
            weigh[8 + 6 * kind + index] = value

    def row(ref, index, line):
        value = ref[index, pl.ds(line, 1), :]
        return jnp.broadcast_to(value, (16, 128)).astype(jnp.bfloat16)[None]

    zero = jnp.zeros((1, 16, 128), jnp.bfloat16)
    count = lax.broadcasted_iota(jnp.int32, (CX // 16, 16, 128), 0) * 16 + lax.broadcasted_iota(jnp.int32, (CX // 16, 16, 128), 1)
    core = (count + 1).astype(jnp.float32).astype(jnp.bfloat16)
    banded = count.astype(jnp.float32).astype(jnp.bfloat16)[: 2 * band // 16]
    sides = lax.broadcasted_iota(jnp.int32, (1, 16, 128), 1)
    side_row = jnp.where(lax.rem(sides, 2) == 0, 0.0, far_x).astype(jnp.bfloat16)
    top = jnp.where(sides < 2, 1.0, 0.0).astype(jnp.bfloat16)

    def hot(ref, line, at=0, rows=core):
        first, second = rows == row(ref, at, line), rows == row(ref, at + 1, line)
        high = jnp.where(first, row(ref, at + 2, line), jnp.where(second, row(ref, at + 4, line), zero))
        low = jnp.where(first, row(ref, at + 3, line), jnp.where(second, row(ref, at + 5, line), zero))
        return high.reshape(-1, 128), low.reshape(-1, 128)

    def across(piece, store):
        for line in range(span):
            store(piece * span + line)

    def build_ghost(kind):
        def store(line):
            high, low = hot(weigh, line, 8 + 6 * kind, banded)
            glhs[kind, line, pl.ds(0, 2 * band)] = high
            glhs[kind, line, pl.ds(2 * band, 2 * band)] = low

        return store

    def build_x(line):
        high, low = hot(rows_x, line)
        xrhs[line, pl.ds(0, CX)] = high
        xrhs[line, pl.ds(CX, CX)] = low
        match = side_row == row(rows_x, 1, line)
        pick = jnp.where(top > zero, row(rows_x, 4, line), row(rows_x, 5, line))
        crhs[line] = jnp.where(match, pick, zero).reshape(16, 128)

    def build_z(line):
        high, low = hot(rows_z, line)
        zrhs[line, pl.ds(0, CZ)] = high
        zrhs[line, pl.ds(CZ, CZ)] = low

    def wide(ref, piece):
        return jnp.concatenate([ref[piece * span + line] for line in range(span)], axis=1)

    def total(terms):
        sums = None
        for term in terms:
            sums = term if sums is None else sums + term
        return sums

    accx[...] = jnp.zeros_like(accx)
    accz[...] = jnp.zeros_like(accz)
    accc[...] = jnp.zeros_like(accc)

    def prepare(piece, carry):
        across(piece, build_x)
        across(piece, build_ghost(0))
        across(piece, build_z)
        across(piece, build_ghost(1))
        accz[...] += nt_dot(wide(glhs.at[0], piece), wide(xrhs, piece))
        accx[...] += nt_dot(wide(glhs.at[1], piece), wide(zrhs, piece))
        accc[...] += nt_dot(wide(glhs.at[0], piece), wide(crhs, piece))
        return carry

    lax.fori_loop(0, pieces, prepare, 0)
    fold_z[:, :CX] = gather(accz[...], 2 * band)
    ends = accc[pl.ds(0, 2 * band)] + accc[pl.ds(2 * band, 2 * band)]
    fold_z[:, CX:] = jnp.zeros((2 * band, CX), jnp.float32)
    fold_z[:, CX : CX + 2] = ends[:, :2] + ends[:, 2:4]
    z_copies = [
        pltpu.make_async_remote_copy(
            src_ref=fold_z.at[pl.ds(side * band, band)],
            dst_ref=zin.at[side],
            send_sem=z_send.at[side],
            recv_sem=z_recv.at[side],
            device_id={"gz": z_next[side]},
            device_id_type=MESH,
        )
        for side in range(2)
    ]

    def paint_rows(first, second):
        for index, y in enumerate((first, second)):
            wy = jnp.where(spot[0] == y, spot[2], jnp.where(spot[1] == y, spot[3], 0.0))
            for place, value in enumerate(parts(spot[4] * wy) + parts(spot[5] * wy)):
                weigh[4 * index + place] = value

        def build(line):
            near, far = core == row(rows_x, 0, line), core == row(rows_x, 1, line)
            for index in range(2):
                for part in range(2):
                    value = jnp.where(near, row(weigh, 4 * index + part, line), jnp.where(far, row(weigh, 4 * index + 2 + part, line), zero))
                    lhs[line, pl.ds((2 * index + part) * CX, CX)] = value.reshape(CX, 128)

        terms = []
        for piece in range(pieces):
            across(piece, build)
            terms.append(nt_dot(wide(lhs, piece), wide(zrhs, piece)))
        sums = total(terms)
        return gather(sums[: 2 * CX], CX), gather(sums[2 * CX :], CX)

    lane = lax.broadcasted_iota(jnp.int32, (CX, CZ), 1)
    band_row = lax.broadcasted_iota(jnp.int32, (2 * CX, band), 1)
    half = groups // 2
    upper = gx // half

    def pencil_of(turn):
        mine = upper * (groups - 1) + (1 - 2 * upper) * gx
        near_by = turn - (groups - half)
        near_by = near_by + jnp.where(near_by >= mine, 1, 0)
        place = jnp.where(turn < groups - half, half + turn, jnp.where(turn == groups - 1, mine, near_by))
        return upper * (groups - 1) + (1 - 2 * upper) * place

    def part_copy(target, part):
        size = CX if part is not YP else 8
        here = pl.ds(pl.multiple_of(part * CX, 8), size)
        return pltpu.make_async_remote_copy(
            src_ref=pen.at[target, here],
            dst_ref=inbox.at[gx, here],
            send_sem=x_send.at[part, target],
            recv_sem=x_recv.at[part, gx],
            device_id={"gx": target},
            device_id_type=MESH,
        )

    y_copies = [
        pltpu.make_async_remote_copy(
            src_ref=yout.at[pl.ds(side * CX, CX)],
            dst_ref=yin.at[side],
            send_sem=y_send.at[side],
            recv_sem=y_recv.at[side],
            device_id={"gy": y_next[side]},
            device_id_type=MESH,
        )
        for side in range(2)
    ] + [
        pltpu.make_async_remote_copy(
            src_ref=yout.at[pl.ds(BODY, 8)],
            dst_ref=yin.at[2 + side, pl.ds(0, 8)],
            send_sem=y_send.at[2 + side],
            recv_sem=y_recv.at[2 + side],
            device_id={"gy": y_next[side]},
            device_id_type=MESH,
        )
        for side in range(2)
    ]
    yout[pl.ds(BODY, 8)] = jnp.zeros((8, CZ), jnp.float32)
    for target in range(groups):
        pen[target, pl.ds(BODY, 8)] = jnp.zeros((8, CZ), jnp.float32)

    def fold_into(target, rows, indices):
        for place, (whole, index) in enumerate(zip(rows, indices)):
            for side, edge_lane in enumerate((CZ - 1, 0)):
                column = jnp.sum(jnp.where(band_row == index, columns[side], 0.0), axis=1, keepdims=True)
                whole = whole + jnp.where(lane == edge_lane, column[:CX], 0.0)
            target[pl.ds(place * CX, CX)] = whole
            for side in range(2):
                target[pl.ds(BODY + 2 * side + place, 1)] = fold_x[side, pl.ds(index, 1)]

    def add_first():
        pen[0, pl.ds(0, CX)] += yin[1]
        for side in range(2):
            pen[0, pl.ds(BODY + 2 * side, 1)] += yin[3, pl.ds(2 * side + 1, 1)]

    def add_last():
        pen[groups - 1, pl.ds((YP - 1) * CX, CX)] += yin[0]
        for side in range(2):
            pen[groups - 1, pl.ds(BODY + 2 * side + YP - 1, 1)] += yin[2, pl.ds(2 * side, 1)]

    late = groups - half

    def visit(turn, carry):
        ghost = turn == 1
        order = jnp.where(turn == 0, 0, turn - 1)
        target = pencil_of(order)
        first = jnp.where(ghost, 0, 1 + target * YP)
        second = jnp.where(ghost, padded_y - 1, 2 + target * YP)
        rows = paint_rows(first.astype(jnp.float32), second.astype(jnp.float32))

        @pl.when(turn == 0)
        def _():
            pl.semaphore_wait(barrier, groups + 3)
            for copy in z_copies:
                copy.start()
            edge = gather(accx[...], 2 * band)
            for copy in z_copies:
                copy.wait()
            edge_lane = lax.broadcasted_iota(jnp.int32, (band, CZ), 1)
            for side in range(2):
                columns[side] = zin[side].T
                part = edge[side * band : (side + 1) * band]
                part = part + jnp.where(edge_lane == CZ - 1, zin[0][:, CX + side : CX + side + 1], 0.0)
                fold_x[side] = part + jnp.where(edge_lane == 0, zin[1][:, CX + side : CX + side + 1], 0.0)

        @pl.when(ghost)
        def _():
            fold_into(yout, rows, (first, second))
            for copy in y_copies:
                copy.start()

        @pl.when(jnp.logical_not(ghost))
        def _():
            fold_into(pen.at[target], rows, (first, second))

            @pl.when(turn > late)
            def _():
                @pl.when(turn == late + 1)
                def _():
                    for copy in y_copies:
                        copy.wait()

                @pl.when(jnp.logical_or(target == 0, jnp.logical_and(turn == late + 1, upper == 1)))
                def _():
                    add_first()

                @pl.when(jnp.logical_or(target == groups - 1, jnp.logical_and(turn == late + 1, upper == 0)))
                def _():
                    add_last()

                @pl.when(turn == late + 1)
                def _():
                    held = (1 - upper) * (groups - 1)
                    part_copy(held, (1 - upper) * (YP - 1)).start()
                    part_copy(held, YP).start()

            @pl.when(turn < groups)
            def _():
                @pl.when(turn == late)
                def _():
                    part_copy(target, upper * (YP - 1)).start()

                @pl.when(turn != late)
                def _():
                    for part in range(YP + 1):
                        part_copy(target, part).start()

        return carry

    lax.fori_loop(0, groups + 1, visit, 0)
    out_ref[gx] = pen[gx]
    for step in range(1, groups):
        source = lax.rem(gx + step, groups)
        for part in range(YP + 1):
            here = pl.ds(part * CX, CX if part < YP else 8)
            part_copy(source, part).wait_send()
            pltpu.make_async_remote_copy(
                src_ref=pen.at[source, here],
                dst_ref=inbox.at[source, here],
                send_sem=x_send.at[part, source],
                recv_sem=x_recv.at[part, source],
                device_id={"gx": source},
                device_id_type=MESH,
            ).wait_recv()
        out_ref[source] = inbox[source]


def paint(dims, cell, offs, mass, live):
    groups = dims[0]
    lines = cell.shape[0]
    band = up(YP * groups + 2, 16)
    vmem = pl.BlockSpec(memory_space=pltpu.VMEM)
    dma = pltpu.SemaphoreType.DMA
    return pl.pallas_call(
        functools.partial(paint_kernel, dims),
        out_shape=jax.ShapeDtypeStruct((groups, ROWS, CZ), jnp.float32),
        in_specs=[pl.BlockSpec(memory_space=pltpu.SMEM), vmem, vmem, vmem],
        out_specs=vmem,
        scratch_shapes=[
            pltpu.VMEM((6, lines, 128), jnp.float32),
            pltpu.VMEM((6, lines, 128), jnp.float32),
            pltpu.VMEM((20, lines, 128), jnp.float32),
            pltpu.VMEM((6, lines, 128), jnp.float32),
            pltpu.VMEM((lines, 2 * CZ, 128), jnp.bfloat16),
            pltpu.VMEM((lines, 2 * CX, 128), jnp.bfloat16),
            pltpu.VMEM((lines, 2 * BODY, 128), jnp.bfloat16),
            pltpu.VMEM((2, lines, 4 * band, 128), jnp.bfloat16),
            pltpu.VMEM((lines, 16, 128), jnp.bfloat16),
            pltpu.VMEM((4 * band, 256), jnp.float32),
            pltpu.VMEM((4 * band, 256), jnp.float32),
            pltpu.VMEM((4 * band, 16), jnp.float32),
            pltpu.VMEM((2, 2 * CX, band), jnp.float32),
            pltpu.VMEM((2, band, CZ), jnp.float32),
            pltpu.VMEM((2 * band, 2 * CX), jnp.float32),
            pltpu.VMEM((2, band, 2 * CX), jnp.float32),
            pltpu.VMEM((ROWS, CZ), jnp.float32),
            pltpu.VMEM((4, CX, CZ), jnp.float32),
            pltpu.VMEM((groups, ROWS, CZ), jnp.float32),
            pltpu.VMEM((groups, ROWS, CZ), jnp.float32),
            dma((2,)),
            dma((2,)),
            dma((4,)),
            dma((4,)),
            dma((YP + 1, groups)),
            dma((YP + 1, groups)),
        ],
        compiler_params=pltpu.CompilerParams(collective_id=0, has_side_effects=True),
    )(live, cell, offs, mass)


def wave_kernel(groups, in_ref, fhi, flo, dens_ref, spec_ref, flat):
    length = groups * CX
    row_id = lax.broadcasted_iota(jnp.int32, (CX, CZ), 0)
    for block in range(groups):
        before, after = (block - 1) % groups, (block + 1) % groups
        for row in range(YP):
            value = in_ref[block, row * CX : (row + 1) * CX]
            upper = BODY + 2 + row
            value = value + jnp.where(row_id == 0, in_ref[before, upper : upper + 1], 0.0)
            lower = BODY + row
            value = value + jnp.where(row_id == CX - 1, in_ref[after, lower : lower + 1], 0.0)
            dens_ref[pl.ds(block * BODY + row, CX, stride=YP), :] = value
            high, low = split(value)
            flat[0, pl.ds(block * CX, CX), pl.ds(row * CZ, CZ)] = high
            flat[1, pl.ds(block * CX, CX), pl.ds(row * CZ, CZ)] = low
    tile = 256

    def transform(turn, carry):
        start = pl.multiple_of(turn * tile, tile)
        rows = pl.ds(start, tile)
        both = jnp.dot(fhi[rows, :], flat[0], preferred_element_type=jnp.float32)
        both += jnp.dot(flo[rows, :], flat[0], preferred_element_type=jnp.float32)
        both += jnp.dot(fhi[rows, :], flat[1], preferred_element_type=jnp.float32)
        for row in range(YP):
            spec_ref[pl.ds(start * YP + row, tile, stride=YP), :] = both[:, row * CZ : (row + 1) * CZ]
        return carry

    lax.fori_loop(0, length // tile, transform, 0)


def waves(groups, pencils):
    length = groups * CX
    half = length // 2
    angle = (np.arange(half)[:, None] * np.arange(length)[None, :] % length) * (2.0 * np.pi / length)
    table = np.concatenate([np.cos(angle), -np.sin(angle)]) / np.sqrt(length)
    fhi = table.astype(jnp.bfloat16)
    flo = (table - fhi.astype(np.float64)).astype(jnp.bfloat16)
    vmem = pl.BlockSpec(memory_space=pltpu.VMEM)
    return pl.pallas_call(
        functools.partial(wave_kernel, groups),
        out_shape=[
            jax.ShapeDtypeStruct((length * YP, CZ), jnp.float32),
            jax.ShapeDtypeStruct((2 * half * YP, CZ), jnp.float32),
        ],
        in_specs=[vmem] * 3,
        out_specs=[vmem] * 2,
        scratch_shapes=[pltpu.VMEM((2, length, YP * CZ), jnp.bfloat16)],
    )(pencils, jnp.asarray(fhi), jnp.asarray(flo))


def body(dims, cell_index, offsets, mass, counts):
    length = dims[0] * CX
    pencils = paint(
        dims, cell_index.reshape(-1, 128), offsets.reshape(3, -1, 128), mass.reshape(-1, 128), counts.reshape(1)
    )
    density, spectrum = waves(dims[0], pencils)
    return (density.reshape(length, 1, YP, CZ), spectrum.reshape(2, length // 2, 1, YP, CZ))


def solution(mesh):
    dims = tuple(mesh.shape[axis] for axis in ("gx", "gy", "gz"))
    placed = (
        P("gx", "gy", "gz", None),
        P("gx", "gy", "gz", None, None),
        P("gx", "gy", "gz", None),
        P("gx", "gy", "gz"),
    )
    return jax.shard_map(
        functools.partial(body, dims),
        mesh=mesh,
        in_specs=placed,
        out_specs=(P(None, "gx", "gy", "gz"), P(None, None, "gx", "gy", "gz")),
        check_vma=False,
    )
```

time: 39.3 us -> 33.9 us (0.86)
  Pallas kernels: 37.9 us -> 32.4 us
    pallas_call x1, Pallas kernels: 34.8 us -> 29.4 us  [paint(): pl.pallas_call(functools.partial(paint_kernel, dims), out_shape=jax.Shape...]
where the time goes in v1:
time: 33.9 us; the launch traced here: 33.7 us
  Pallas kernels  32.4 us (96%)
  between operations  1.28 us (4%)
    pallas_call x1, Pallas kernels, paint(): pl.pallas_call(functools.partial(paint_kernel, dims), out_shape=jax.Shape...  29.4 us
    pallas_call x1, Pallas kernels, waves(): pl.pallas_call(functools.partial(wave_kernel, groups), out_shape=[jax.Sha...  3.03 us

profile of v1, /device:TPU:0, one launch (start us, length us, event | category | flops | bytes accessed | tf_op | source)
XLA Modules:
  0.0 33.7 jit_solution(17818375581257255030)
XLA Ops:
  1.3 29.4 %shard_map.77.in_ref = f32[4,264,128]{2,1,0:T(8,128)} custom-call(s32[1]{0:T(128)} %bitcast.10.live_ref, s32[64,128]{1,0:T(8,128)} %bitcast.12, f32[3,64,128]{2,1,0:T(8,128)} %bitcast.11, f32[64,128]{1,0:T(8,128)} %bitcast.13), custom_call_target="tpu_custom_call" | custom-call | tf_op jit(solution)/shard_map/pallas_call | solution.py:361
  30.7 3.0 %shard_map.78 = (f32[1024,128]{1,0:T(8,128)}, f32[1024,128]{1,0:T(8,128)}) custom-call(f32[4,264,128]{2,1,0:T(8,128)} %shard_map.77.in_ref, bf16[512,512]{1,0:T(8,128)(2,1)} %constant.4.clone.fhi, bf16[512,512]{1,0:T(8,128)(2,1)} %constant.5.clone.flo), custom_call_target="tpu_custom_call" | custom-call | tf_op jit(solution)/shard_map/pallas_call | solution.py:436

commit v2 on v1

--- a/solution.py
+++ b/solution.py
@@ -42,10 +42,16 @@
     return high, value - high
 
 
-def paint_kernel(dims, live_ref, cell_ref, off_ref, mass_ref, out_ref, rows_x, rows_z, weigh, spot, zrhs, xrhs, lhs, glhs, crhs, accx, accz, accc, columns, fold_x, fold_z, zin, yout, yin, pen, inbox, z_send, z_recv, y_send, y_recv, x_send, x_recv):
+def paint_kernel(dims, live_ref, cell_hbm, off_hbm, mass_hbm, out_ref, cell_ref, off_ref, mass_ref, rows_x, rows_z, weigh, spot, zrhs, xrhs, lhs, glhs, crhs, accz, accc, columns, corner, fold_z, zin, yout, yin, pen, load, z_send, z_recv, y_send, y_recv, x_send, x_recv):
     groups, count_y, count_z = dims
     padded_y = YP * groups + 2
     band = up(padded_y, 16)
+    loads = [
+        pltpu.make_async_copy(source, target, load.at[index])
+        for index, (source, target) in enumerate(((cell_hbm, cell_ref), (off_hbm, off_ref), (mass_hbm, mass_ref)))
+    ]
+    for copy in loads:
+        copy.start()
     stride_y = CZ + 2
     stride_x = padded_y * stride_y
     lines = cell_ref.shape[0]
@@ -62,6 +68,8 @@
     for step in range(1, groups):
         pl.semaphore_signal(barrier, inc=1, device_id={"gx": lax.rem(gx + step, groups)}, device_id_type=MESH)
 
+    for copy in loads:
+        copy.wait()
     live = live_ref[0]
     slot = lax.broadcasted_iota(jnp.int32, (lines, 128), 0) * 128 + lax.broadcasted_iota(jnp.int32, (lines, 128), 1)
     loaded = jnp.where(slot < live, mass_ref[...], 0.0)
@@ -84,15 +92,10 @@
     for index, value in enumerate((z0, z1) + parts(ez) + parts(fz)):
         rows_z[index] = value
     far_x, far_z = CX + 1.0, CZ + 1.0
-    gx_y = jnp.where(x1 == 0.0, 0.0, jnp.where(x1 == far_x, float(band), -1.0 - band))
     gz_y = jnp.where(z1 == 0.0, 0.0, jnp.where(z1 == far_z, float(band), -1.0 - band))
-    ghost_rows = (
-        (gz_y + y0, gz_y + y1) + parts(fz * my0) + parts(fz * my1),
-        (gx_y + y0, gx_y + y1) + parts(fx * my0) + parts(fx * my1),
-    )
-    for kind in range(2):
-        for index, value in enumerate(ghost_rows[kind]):
-            weigh[8 + 6 * kind + index] = value
+    ghost_rows = (gz_y + y0, gz_y + y1) + parts(fz * my0) + parts(fz * my1)
+    for index, value in enumerate(ghost_rows):
+        weigh[8 + index] = value
 
     def row(ref, index, line):
         value = ref[index, pl.ds(line, 1), :]
@@ -103,6 +106,8 @@
     core = (count + 1).astype(jnp.float32).astype(jnp.bfloat16)
     banded = count.astype(jnp.float32).astype(jnp.bfloat16)[: 2 * band // 16]
     sides = lax.broadcasted_iota(jnp.int32, (1, 16, 128), 1)
+    edge_row = jnp.where(sides < 4 * YP, jnp.where(lax.rem(sides, 2) == 0, 0.0, far_x), -9.0).astype(jnp.bfloat16)
+    level = sides.astype(jnp.float32).astype(jnp.bfloat16)
     side_row = jnp.where(lax.rem(sides, 2) == 0, 0.0, far_x).astype(jnp.bfloat16)
     top = jnp.where(sides < 2, 1.0, 0.0).astype(jnp.bfloat16)
 
@@ -116,13 +121,10 @@
         for line in range(span):
             store(piece * span + line)
 
-    def build_ghost(kind):
-        def store(line):
-            high, low = hot(weigh, line, 8 + 6 * kind, banded)
-            glhs[kind, line, pl.ds(0, 2 * band)] = high
-            glhs[kind, line, pl.ds(2 * band, 2 * band)] = low
-
-        return store
+    def build_ghost(line):
+        high, low = hot(weigh, line, 8, banded)
+        glhs[line, pl.ds(0, 2 * band)] = high
+        glhs[line, pl.ds(2 * band, 2 * band)] = low
 
     def build_x(line):
         high, low = hot(rows_x, line)
@@ -137,8 +139,8 @@
         zrhs[line, pl.ds(0, CZ)] = high
         zrhs[line, pl.ds(CZ, CZ)] = low
 
-    def wide(ref, piece):
-        return jnp.concatenate([ref[piece * span + line] for line in range(span)], axis=1)
+    def wide(ref, start, width):
+        return jnp.concatenate([ref[start + line] for line in range(width)], axis=1)
 
     def total(terms):
         sums = None
@@ -146,22 +148,22 @@
             sums = term if sums is None else sums + term
         return sums
 
-    accx[...] = jnp.zeros_like(accx)
     accz[...] = jnp.zeros_like(accz)
     accc[...] = jnp.zeros_like(accc)
+    step = span // 2
 
     def prepare(piece, carry):
         across(piece, build_x)
-        across(piece, build_ghost(0))
+        across(piece, build_ghost)
         across(piece, build_z)
-        across(piece, build_ghost(1))
-        accz[...] += nt_dot(wide(glhs.at[0], piece), wide(xrhs, piece))
-        accx[...] += nt_dot(wide(glhs.at[1], piece), wide(zrhs, piece))
-        accc[...] += nt_dot(wide(glhs.at[0], piece), wide(crhs, piece))
+        for side in range(2):
+            start = piece * span + side * step
+            accz[side] += nt_dot(wide(glhs, start, step), wide(xrhs, start, step))
+        accc[...] += nt_dot(wide(glhs, piece * span, span), wide(crhs, piece * span, span))
         return carry
 
     lax.fori_loop(0, pieces, prepare, 0)
-    fold_z[:, :CX] = gather(accz[...], 2 * band)
+    fold_z[:, :CX] = gather(accz[0] + accz[1], 2 * band)
     ends = accc[pl.ds(0, 2 * band)] + accc[pl.ds(2 * band, 2 * band)]
     fold_z[:, CX:] = jnp.zeros((2 * band, CX), jnp.float32)
     fold_z[:, CX : CX + 2] = ends[:, :2] + ends[:, 2:4]
@@ -176,6 +178,9 @@
         )
         for side in range(2)
     ]
+    pl.semaphore_wait(barrier, groups + 3)
+    for copy in z_copies:
+        copy.start()
 
     def paint_rows(first, second):
         for index, y in enumerate((first, second)):
@@ -189,16 +194,23 @@
                 for part in range(2):
                     value = jnp.where(near, row(weigh, 4 * index + part, line), jnp.where(far, row(weigh, 4 * index + 2 + part, line), zero))
                     lhs[line, pl.ds((2 * index + part) * CX, CX)] = value.reshape(CX, 128)
+            pick = zero
+            for index in reversed(range(4)):
+                pick = jnp.where(level < jnp.bfloat16(2 * index + 2), row(weigh, 4 * (index // 2) + 2 + index % 2, line), pick)
+            pick = jnp.where(edge_row == row(rows_x, 1, line), pick, zero)
+            lhs[line, pl.ds(2 * BODY, 16)] = pick.reshape(16, 128)
 
         terms = []
         for piece in range(pieces):
             across(piece, build)
-            terms.append(nt_dot(wide(lhs, piece), wide(zrhs, piece)))
+            terms.append(nt_dot(wide(lhs, piece * span, span), wide(zrhs, piece * span, span)))
         sums = total(terms)
-        return gather(sums[: 2 * CX], CX), gather(sums[2 * CX :], CX)
+        edges = sums[2 * BODY :, :128] + sums[2 * BODY :, 128:]
+        return gather(sums[: 2 * CX], CX), gather(sums[2 * CX : 2 * BODY], CX), edges
 
     lane = lax.broadcasted_iota(jnp.int32, (CX, CZ), 1)
-    band_row = lax.broadcasted_iota(jnp.int32, (2 * CX, band), 1)
+    band_row = lax.broadcasted_iota(jnp.int32, (CX, band), 1)
+    edge_lane = lax.broadcasted_iota(jnp.int32, (1, CZ), 1)
     half = groups // 2
     upper = gx // half
 
@@ -214,7 +226,7 @@
         here = pl.ds(pl.multiple_of(part * CX, 8), size)
         return pltpu.make_async_remote_copy(
             src_ref=pen.at[target, here],
-            dst_ref=inbox.at[gx, here],
+            dst_ref=out_ref.at[gx, here],
             send_sem=x_send.at[part, target],
             recv_sem=x_recv.at[part, gx],
             device_id={"gx": target},
@@ -247,13 +259,20 @@
         pen[target, pl.ds(BODY, 8)] = jnp.zeros((8, CZ), jnp.float32)
 
     def fold_into(target, rows, indices):
-        for place, (whole, index) in enumerate(zip(rows, indices)):
-            for side, edge_lane in enumerate((CZ - 1, 0)):
-                column = jnp.sum(jnp.where(band_row == index, columns[side], 0.0), axis=1, keepdims=True)
-                whole = whole + jnp.where(lane == edge_lane, column[:CX], 0.0)
-            target[pl.ds(place * CX, CX)] = whole
+        edges = rows[2]
+        for place, index in enumerate(indices):
+            sides = [
+                jnp.sum(jnp.where(band_row == index, columns[side], 0.0), axis=1, keepdims=True) for side in range(2)
+            ]
+            ghosts = jnp.where(lane == CZ - 1, sides[0], jnp.where(lane == 0, sides[1], 0.0))
+            target[pl.ds(place * CX, CX)] = rows[place] + ghosts
+            ends = [corner[side, pl.ds(index, 1)] for side in range(2)]
             for side in range(2):
-                target[pl.ds(BODY + 2 * side + place, 1)] = fold_x[side, pl.ds(index, 1)]
+                at = 4 * place + side
+                value = edges[at : at + 1] + edges[at + 2 : at + 3]
+                value = value + jnp.where(edge_lane == CZ - 1, ends[0][:, side : side + 1], 0.0)
+                value = value + jnp.where(edge_lane == 0, ends[1][:, side : side + 1], 0.0)
+                target[pl.ds(BODY + 2 * side + place, 1)] = value
 
     def add_first():
         pen[0, pl.ds(0, CX)] += yin[1]
@@ -277,18 +296,11 @@
 
         @pl.when(turn == 0)
         def _():
-            pl.semaphore_wait(barrier, groups + 3)
-            for copy in z_copies:
-                copy.start()
-            edge = gather(accx[...], 2 * band)
             for copy in z_copies:
                 copy.wait()
-            edge_lane = lax.broadcasted_iota(jnp.int32, (band, CZ), 1)
             for side in range(2):
-                columns[side] = zin[side].T
-                part = edge[side * band : (side + 1) * band]
-                part = part + jnp.where(edge_lane == CZ - 1, zin[0][:, CX + side : CX + side + 1], 0.0)
-                fold_x[side] = part + jnp.where(edge_lane == 0, zin[1][:, CX + side : CX + side + 1], 0.0)
+                columns[side] = zin[side, :, pl.ds(0, CX)].T
+                corner[side] = zin[side, :, pl.ds(CX, CX)]
 
         @pl.when(ghost)
         def _():
@@ -343,47 +355,49 @@
             part_copy(source, part).wait_send()
             pltpu.make_async_remote_copy(
                 src_ref=pen.at[source, here],
-                dst_ref=inbox.at[source, here],
+                dst_ref=out_ref.at[source, here],
                 send_sem=x_send.at[part, source],
                 recv_sem=x_recv.at[part, source],
                 device_id={"gx": source},
                 device_id_type=MESH,
             ).wait_recv()
-        out_ref[source] = inbox[source]
 
 
 def paint(dims, cell, offs, mass, live):
     groups = dims[0]
     lines = cell.shape[0]
     band = up(YP * groups + 2, 16)
+    work = 2 * (YP * groups + 2) * 4 * CX * CZ * lines * 128
     vmem = pl.BlockSpec(memory_space=pltpu.VMEM)
     dma = pltpu.SemaphoreType.DMA
     return pl.pallas_call(
         functools.partial(paint_kernel, dims),
         out_shape=jax.ShapeDtypeStruct((groups, ROWS, CZ), jnp.float32),
-        in_specs=[pl.BlockSpec(memory_space=pltpu.SMEM), vmem, vmem, vmem],
+        in_specs=[pl.BlockSpec(memory_space=pltpu.SMEM)] + [pl.BlockSpec(memory_space=pltpu.HBM)] * 3,
         out_specs=vmem,
         scratch_shapes=[
+            pltpu.VMEM((lines, 128), jnp.int32),
+            pltpu.VMEM((3, lines, 128), jnp.float32),
+            pltpu.VMEM((lines, 128), jnp.float32),
             pltpu.VMEM((6, lines, 128), jnp.float32),
             pltpu.VMEM((6, lines, 128), jnp.float32),
-            pltpu.VMEM((20, lines, 128), jnp.float32),
+            pltpu.VMEM((14, lines, 128), jnp.float32),
             pltpu.VMEM((6, lines, 128), jnp.float32),
             pltpu.VMEM((lines, 2 * CZ, 128), jnp.bfloat16),
             pltpu.VMEM((lines, 2 * CX, 128), jnp.bfloat16),
-            pltpu.VMEM((lines, 2 * BODY, 128), jnp.bfloat16),
-            pltpu.VMEM((2, lines, 4 * band, 128), jnp.bfloat16),
+            pltpu.VMEM((lines, 2 * BODY + 16, 128), jnp.bfloat16),
+            pltpu.VMEM((lines, 4 * band, 128), jnp.bfloat16),
             pltpu.VMEM((lines, 16, 128), jnp.bfloat16),
-            pltpu.VMEM((4 * band, 256), jnp.float32),
-            pltpu.VMEM((4 * band, 256), jnp.float32),
+            pltpu.VMEM((2, 4 * band, 256), jnp.float32),
             pltpu.VMEM((4 * band, 16), jnp.float32),
-            pltpu.VMEM((2, 2 * CX, band), jnp.float32),
-            pltpu.VMEM((2, band, CZ), jnp.float32),
+            pltpu.VMEM((2, CX, band), jnp.float32),
+            pltpu.VMEM((2, band, CX), jnp.float32),
             pltpu.VMEM((2 * band, 2 * CX), jnp.float32),
             pltpu.VMEM((2, band, 2 * CX), jnp.float32),
             pltpu.VMEM((ROWS, CZ), jnp.float32),
             pltpu.VMEM((4, CX, CZ), jnp.float32),
             pltpu.VMEM((groups, ROWS, CZ), jnp.float32),
-            pltpu.VMEM((groups, ROWS, CZ), jnp.float32),
+            dma((3,)),
             dma((2,)),
             dma((2,)),
             dma((4,)),
@@ -391,11 +405,14 @@
             dma((YP + 1, groups)),
             dma((YP + 1, groups)),
         ],
-        compiler_params=pltpu.CompilerParams(collective_id=0, has_side_effects=True),
-    )(live, cell, offs, mass)
-
-
-def wave_kernel(groups, in_ref, fhi, flo, dens_ref, spec_ref, flat):
+        cost_estimate=pl.CostEstimate(flops=work, bytes_accessed=24 * lines * 128, transcendentals=0),
+        compiler_params=pltpu.CompilerParams(
+            collective_id=0, has_side_effects=True, vmem_limit_bytes=32 * 1024 * 1024
+        ),
+    )(live, *(pltpu.with_memory_space_constraint(value, pltpu.HBM) for value in (cell, offs, mass)))
+
+
+def wave_kernel(groups, in_ref, table, dens_ref, spec_ref, flat):
     length = groups * CX
     row_id = lax.broadcasted_iota(jnp.int32, (CX, CZ), 0)
     for block in range(groups):
@@ -415,9 +432,9 @@
     def transform(turn, carry):
         start = pl.multiple_of(turn * tile, tile)
         rows = pl.ds(start, tile)
-        both = jnp.dot(fhi[rows, :], flat[0], preferred_element_type=jnp.float32)
-        both += jnp.dot(flo[rows, :], flat[0], preferred_element_type=jnp.float32)
-        both += jnp.dot(fhi[rows, :], flat[1], preferred_element_type=jnp.float32)
+        both = jnp.dot(table[0, rows, :], flat[0], preferred_element_type=jnp.float32)
+        both += jnp.dot(table[1, rows, :], flat[0], preferred_element_type=jnp.float32)
+        both += jnp.dot(table[0, rows, :], flat[1], preferred_element_type=jnp.float32)
         for row in range(YP):
             spec_ref[pl.ds(start * YP + row, tile, stride=YP), :] = both[:, row * CZ : (row + 1) * CZ]
         return carry
@@ -439,10 +456,11 @@
             jax.ShapeDtypeStruct((length * YP, CZ), jnp.float32),
             jax.ShapeDtypeStruct((2 * half * YP, CZ), jnp.float32),
         ],
-        in_specs=[vmem] * 3,
+        in_specs=[vmem] * 2,
         out_specs=[vmem] * 2,
         scratch_shapes=[pltpu.VMEM((2, length, YP * CZ), jnp.bfloat16)],
-    )(pencils, jnp.asarray(fhi), jnp.asarray(flo))
+        compiler_params=pltpu.CompilerParams(vmem_limit_bytes=24 * 1024 * 1024),
+    )(pencils, jnp.asarray(np.stack([fhi, flo])))
 
 
 def body(dims, cell_index, offsets, mass, counts):

time: 33.9 us -> 29.9 us (0.88)
  Pallas kernels: 32.4 us -> 28.5 us
    pallas_call x1, Pallas kernels: 29.4 us -> 26.8 us  [paint(): pl.pallas_call(functools.partial(paint_kernel, dims), out_shape=jax.Shape...]
    pallas_call x1, Pallas kernels: 3.03 us -> 1.66 us  [waves(): pl.pallas_call(functools.partial(wave_kernel, groups), out_shape=[jax.Sha...]
where the time goes in v2:
time: 29.9 us; the launch traced here: 29.8 us
  Pallas kernels  28.5 us (95%)
  between operations  1.3 us (4%)
    pallas_call x1, Pallas kernels, paint(): pl.pallas_call(functools.partial(paint_kernel, dims), out_shape=jax.Shape...  26.8 us
    pallas_call x1, Pallas kernels, waves(): pl.pallas_call(functools.partial(wave_kernel, groups), out_shape=[jax.Sha...  1.66 us

profile of v2, /device:TPU:0, one launch (start us, length us, event | category | flops | bytes accessed | tf_op | source)
XLA Modules:
  0.0 29.8 jit_solution(12630670854794502857)
XLA Ops:
  1.3 0.0 copy-start
  1.3 26.8 %shard_map.68.in_ref = f32[4,264,128]{2,1,0:T(8,128)S(1)} custom-call(s32[1]{0:T(128)} %bitcast.10.live_ref, s32[64,128]{1,0:T(8,128)} %bitcast.14, f32[3,64,128]{2,1,0:T(8,128)} %bitcast.13, f32[64,128]{1,0:T(8,128)} %bitcast.15), custom_call_target="tpu_custom_call" | custom-call | flops 10737418240 | bytes 196608 | tf_op jit(solution)/shard_map/pallas_call | solution.py:373
  28.1 0.0 copy-done
  28.1 1.7 %shard_map.69 = (f32[1024,128]{1,0:T(8,128)}, f32[1024,128]{1,0:T(8,128)}) custom-call(f32[4,264,128]{2,1,0:T(8,128)S(1)} %shard_map.68.in_ref, bf16[2,512,512]{2,1,0:T(8,128)(2,1)S(1)} %copy-done), custom_call_target="tpu_custom_call" | custom-call | tf_op jit(solution)/shard_map/pallas_call | solution.py:453
Async XLA Ops:
  1.3 26.8 %copy-start = (bf16[2,512,512]{2,1,0:T(8,128)(2,1)S(1)}, bf16[2,512,512]{2,1,0:T(8,128)(2,1)}, u32[]{:S(2)}) copy-start(bf16[2,512,512]{2,1,0:T(8,128)(2,1)} %constant.2.clone.table) | copy-start | bytes 3145732

commit v3 on v2

--- a/solution.py
+++ b/solution.py
@@ -42,7 +42,7 @@
     return high, value - high
 
 
-def paint_kernel(dims, live_ref, cell_hbm, off_hbm, mass_hbm, out_ref, cell_ref, off_ref, mass_ref, rows_x, rows_z, weigh, spot, zrhs, xrhs, lhs, glhs, crhs, accz, accc, columns, corner, fold_z, zin, yout, yin, pen, load, z_send, z_recv, y_send, y_recv, x_send, x_recv):
+def paint_kernel(dims, live_ref, cell_hbm, off_hbm, mass_hbm, out_ref, cell_ref, off_ref, mass_ref, rows_x, rows_z, weigh, spot, zrhs, xrhs, lhs, glhs, crhs, fold_z, zin, yout, yin, pen, load, z_send, z_recv, y_send, y_recv, x_send, x_recv):
     groups, count_y, count_z = dims
     padded_y = YP * groups + 2
     band = up(padded_y, 16)
@@ -148,40 +148,6 @@
             sums = term if sums is None else sums + term
         return sums
 
-    accz[...] = jnp.zeros_like(accz)
-    accc[...] = jnp.zeros_like(accc)
-    step = span // 2
-
-    def prepare(piece, carry):
-        across(piece, build_x)
-        across(piece, build_ghost)
-        across(piece, build_z)
-        for side in range(2):
-            start = piece * span + side * step
-            accz[side] += nt_dot(wide(glhs, start, step), wide(xrhs, start, step))
-        accc[...] += nt_dot(wide(glhs, piece * span, span), wide(crhs, piece * span, span))
-        return carry
-
-    lax.fori_loop(0, pieces, prepare, 0)
-    fold_z[:, :CX] = gather(accz[0] + accz[1], 2 * band)
-    ends = accc[pl.ds(0, 2 * band)] + accc[pl.ds(2 * band, 2 * band)]
-    fold_z[:, CX:] = jnp.zeros((2 * band, CX), jnp.float32)
-    fold_z[:, CX : CX + 2] = ends[:, :2] + ends[:, 2:4]
-    z_copies = [
-        pltpu.make_async_remote_copy(
-            src_ref=fold_z.at[pl.ds(side * band, band)],
-            dst_ref=zin.at[side],
-            send_sem=z_send.at[side],
-            recv_sem=z_recv.at[side],
-            device_id={"gz": z_next[side]},
-            device_id_type=MESH,
-        )
-        for side in range(2)
-    ]
-    pl.semaphore_wait(barrier, groups + 3)
-    for copy in z_copies:
-        copy.start()
-
     def paint_rows(first, second):
         for index, y in enumerate((first, second)):
             wy = jnp.where(spot[0] == y, spot[2], jnp.where(spot[1] == y, spot[3], 0.0))
@@ -208,8 +174,6 @@
         edges = sums[2 * BODY :, :128] + sums[2 * BODY :, 128:]
         return gather(sums[: 2 * CX], CX), gather(sums[2 * CX : 2 * BODY], CX), edges
 
-    lane = lax.broadcasted_iota(jnp.int32, (CX, CZ), 1)
-    band_row = lax.broadcasted_iota(jnp.int32, (CX, band), 1)
     edge_lane = lax.broadcasted_iota(jnp.int32, (1, CZ), 1)
     half = groups // 2
     upper = gx // half
@@ -254,99 +218,158 @@
         )
         for side in range(2)
     ]
-    yout[pl.ds(BODY, 8)] = jnp.zeros((8, CZ), jnp.float32)
-    for target in range(groups):
-        pen[target, pl.ds(BODY, 8)] = jnp.zeros((8, CZ), jnp.float32)
-
-    def fold_into(target, rows, indices):
-        edges = rows[2]
-        for place, index in enumerate(indices):
-            sides = [
-                jnp.sum(jnp.where(band_row == index, columns[side], 0.0), axis=1, keepdims=True) for side in range(2)
-            ]
-            ghosts = jnp.where(lane == CZ - 1, sides[0], jnp.where(lane == 0, sides[1], 0.0))
-            target[pl.ds(place * CX, CX)] = rows[place] + ghosts
-            ends = [corner[side, pl.ds(index, 1)] for side in range(2)]
-            for side in range(2):
-                at = 4 * place + side
-                value = edges[at : at + 1] + edges[at + 2 : at + 3]
-                value = value + jnp.where(edge_lane == CZ - 1, ends[0][:, side : side + 1], 0.0)
-                value = value + jnp.where(edge_lane == 0, ends[1][:, side : side + 1], 0.0)
-                target[pl.ds(BODY + 2 * side + place, 1)] = value
+    def put(target, place, rows, at):
+        edges = rows[YP]
+        target[pl.ds(pl.multiple_of(place * CX, 8), CX)] = rows[at]
+        for side in range(2):
+            low = 4 * at + side
+            target[pl.ds(BODY + 2 * side + place, 1)] = edges[low : low + 1] + edges[low + 2 : low + 3]
+
+    def finish(target, place, index):
+        ends = [zin[side, 1, pl.ds(index, 1)] for side in range(2)]
+        for side in range(2):
+            extra = jnp.where(edge_lane == CZ - 1, ends[0][:, side : side + 1], 0.0)
+            extra = extra + jnp.where(edge_lane == 0, ends[1][:, side : side + 1], 0.0)
+            target[pl.ds(BODY + 2 * side + place, 1)] += extra
+            target[pl.ds(BODY + 4 + 2 * side + place, 1)] = zin[side, 0, pl.ds(index, 1)]
 
     def add_first():
         pen[0, pl.ds(0, CX)] += yin[1]
-        for side in range(2):
-            pen[0, pl.ds(BODY + 2 * side, 1)] += yin[3, pl.ds(2 * side + 1, 1)]
+        for kind in range(4):
+            pen[0, pl.ds(BODY + 2 * kind, 1)] += yin[3, pl.ds(2 * kind + 1, 1)]
 
     def add_last():
         pen[groups - 1, pl.ds((YP - 1) * CX, CX)] += yin[0]
+        for kind in range(4):
+            pen[groups - 1, pl.ds(BODY + 2 * kind + YP - 1, 1)] += yin[2, pl.ds(2 * kind, 1)]
+
+    late = groups - half
+
+    def line_of(target, place):
+        return 1 + target * YP + place
+
+    def as_float(indices):
+        return [index.astype(jnp.float32) for index in indices]
+
+    def build_all(piece, carry):
+        across(piece, build_z)
+        return carry
+
+    lax.fori_loop(0, pieces, build_all, 0)
+    leader = pencil_of(jnp.int32(0))
+    rows = paint_rows(*as_float([line_of(leader, place) for place in range(YP)]))
+    for place in range(YP):
+        put(pen.at[leader], place, rows, place)
+    pl.semaphore_wait(barrier, groups + 3)
+    for part in range(YP):
+        part_copy(leader, part).start()
+
+    z_copies = [
+        pltpu.make_async_remote_copy(
+            src_ref=fold_z.at[side],
+            dst_ref=zin.at[side],
+            send_sem=z_send.at[side],
+            recv_sem=z_recv.at[side],
+            device_id={"gz": z_next[side]},
+            device_id_type=MESH,
+        )
+        for side in range(2)
+    ]
+    def send_ghosts():
+        step = pieces // 2
+        sums = []
+        for piece in range(pieces):
+            across(piece, build_x)
+            across(piece, build_ghost)
         for side in range(2):
-            pen[groups - 1, pl.ds(BODY + 2 * side + YP - 1, 1)] += yin[2, pl.ds(2 * side, 1)]
-
-    late = groups - half
+            starts = [piece * span for piece in range(side * step, step if side == 0 else pieces)]
+            sums.append(total(nt_dot(wide(glhs, start, span), wide(xrhs, start, span)) for start in starts))
+        ends = total(nt_dot(wide(glhs, piece * span, span), wide(crhs, piece * span, span)) for piece in range(pieces))
+        sums = gather(sums[0] + sums[1], 2 * band)
+        ends = ends[: 2 * band] + ends[2 * band :]
+        ends = ends[:, :2] + ends[:, 2:4]
+        for side in range(2):
+            here = slice(side * band, side * band + band)
+            fold_z[side, 0] = sums[here]
+            fold_z[side, 1] = jnp.zeros((band, CX), jnp.float32)
+            fold_z[side, 1, :, pl.ds(0, 2)] = ends[here]
+        for copy in z_copies:
+            copy.start()
+
+    pl.when(gx >= 0)(send_ghosts)
+    held, close = pencil_of(jnp.int32(late - 1)), pencil_of(jnp.int32(late))
 
     def visit(turn, carry):
         ghost = turn == 1
-        order = jnp.where(turn == 0, 0, turn - 1)
-        target = pencil_of(order)
-        first = jnp.where(ghost, 0, 1 + target * YP)
-        second = jnp.where(ghost, padded_y - 1, 2 + target * YP)
-        rows = paint_rows(first.astype(jnp.float32), second.astype(jnp.float32))
-
-        @pl.when(turn == 0)
+        whole = pencil_of(turn - 1)
+        early, second = turn == late, turn == late + 1
+        split_turn = jnp.logical_or(early, second)
+        targets = (jnp.where(split_turn, held, whole), jnp.where(split_turn, close, whole))
+        places = (
+            jnp.where(early, upper, jnp.where(second, 1 - upper, 0)),
+            jnp.where(early, 1 - upper, jnp.where(second, upper, 1)),
+        )
+        lines = [line_of(target, place) for target, place in zip(targets, places)]
+        lines = (jnp.where(ghost, 0, lines[0]), jnp.where(ghost, padded_y - 1, lines[1]))
+        rows = paint_rows(*as_float(lines))
+
+        @pl.when(ghost)
         def _():
+            for place in range(YP):
+                put(yout, place, rows, place)
             for copy in z_copies:
                 copy.wait()
-            for side in range(2):
-                columns[side] = zin[side, :, pl.ds(0, CX)].T
-                corner[side] = zin[side, :, pl.ds(CX, CX)]
-
-        @pl.when(ghost)
-        def _():
-            fold_into(yout, rows, (first, second))
+            for place, line in enumerate(lines):
+                finish(yout, place, line)
             for copy in y_copies:
                 copy.start()
+            for place in range(YP):
+                finish(pen.at[leader], place, line_of(leader, place))
+            part_copy(leader, YP).start()
 
         @pl.when(jnp.logical_not(ghost))
         def _():
-            fold_into(pen.at[target], rows, (first, second))
-
-            @pl.when(turn > late)
+            for at, (target, place) in enumerate(zip(targets, places)):
+                put(pen.at[target], place, rows, at)
+
+            @pl.when(early)
             def _():
-                @pl.when(turn == late + 1)
-                def _():
-                    for copy in y_copies:
-                        copy.wait()
-
-                @pl.when(jnp.logical_or(target == 0, jnp.logical_and(turn == late + 1, upper == 1)))
-                def _():
-                    add_first()
-
-                @pl.when(jnp.logical_or(target == groups - 1, jnp.logical_and(turn == late + 1, upper == 0)))
-                def _():
-                    add_last()
-
-                @pl.when(turn == late + 1)
-                def _():
-                    held = (1 - upper) * (groups - 1)
-                    part_copy(held, (1 - upper) * (YP - 1)).start()
-                    part_copy(held, YP).start()
-
-            @pl.when(turn < groups)
+                for target, place in zip(targets, places):
+                    part_copy(target, place).start()
+
+            for target, place, line in zip(targets, places, lines):
+                finish(pen.at[target], place, line)
+
+            @pl.when(second)
             def _():
-                @pl.when(turn == late)
-                def _():
-                    part_copy(target, upper * (YP - 1)).start()
-
-                @pl.when(turn != late)
-                def _():
-                    for part in range(YP + 1):
-                        part_copy(target, part).start()
+                for copy in y_copies:
+                    copy.wait()
+
+            @pl.when(jnp.logical_or(jnp.logical_and(second, gx != 0), jnp.logical_and(turn == groups, gx == 0)))
+            def _():
+                add_first()
+
+            @pl.when(
+                jnp.logical_or(
+                    jnp.logical_and(second, gx != groups - 1), jnp.logical_and(turn == groups, gx == groups - 1)
+                )
+            )
+            def _():
+                add_last()
+
+            @pl.when(jnp.logical_and(turn < groups, jnp.logical_not(early)))
+            def _():
+                for target, place in zip(targets, places):
+                    part_copy(target, place).start()
+                part_copy(targets[0], YP).start()
+
+            @pl.when(second)
+            def _():
+                part_copy(close, YP).start()
 
         return carry
 
-    lax.fori_loop(0, groups + 1, visit, 0)
+    lax.fori_loop(1, groups + 1, visit, 0)
     out_ref[gx] = pen[gx]
     for step in range(1, groups):
         source = lax.rem(gx + step, groups)
@@ -388,12 +411,8 @@
             pltpu.VMEM((lines, 2 * BODY + 16, 128), jnp.bfloat16),
             pltpu.VMEM((lines, 4 * band, 128), jnp.bfloat16),
             pltpu.VMEM((lines, 16, 128), jnp.bfloat16),
-            pltpu.VMEM((2, 4 * band, 256), jnp.float32),
-            pltpu.VMEM((4 * band, 16), jnp.float32),
-            pltpu.VMEM((2, CX, band), jnp.float32),
-            pltpu.VMEM((2, band, CX), jnp.float32),
-            pltpu.VMEM((2 * band, 2 * CX), jnp.float32),
-            pltpu.VMEM((2, band, 2 * CX), jnp.float32),
+            pltpu.VMEM((2, 2, band, CX), jnp.float32),
+            pltpu.VMEM((2, 2, band, CX), jnp.float32),
             pltpu.VMEM((ROWS, CZ), jnp.float32),
             pltpu.VMEM((4, CX, CZ), jnp.float32),
             pltpu.VMEM((groups, ROWS, CZ), jnp.float32),
@@ -415,6 +434,8 @@
 def wave_kernel(groups, in_ref, table, dens_ref, spec_ref, flat):
     length = groups * CX
     row_id = lax.broadcasted_iota(jnp.int32, (CX, CZ), 0)
+    lane = lax.broadcasted_iota(jnp.int32, (CX, CZ), 1)
+    columns = jnp.concatenate([in_ref[block, BODY:ROWS] for block in range(groups)], axis=0).T
     for block in range(groups):
         before, after = (block - 1) % groups, (block + 1) % groups
         for row in range(YP):
@@ -423,6 +444,8 @@
             value = value + jnp.where(row_id == 0, in_ref[before, upper : upper + 1], 0.0)
             lower = BODY + row
             value = value + jnp.where(row_id == CX - 1, in_ref[after, lower : lower + 1], 0.0)
+            ends = [columns[:, 8 * block + 4 + 2 * side + row :][:, :1] for side in range(2)]
+            value = value + jnp.where(lane == CZ - 1, ends[0], jnp.where(lane == 0, ends[1], 0.0))
             dens_ref[pl.ds(block * BODY + row, CX, stride=YP), :] = value
             high, low = split(value)
             flat[0, pl.ds(block * CX, CX), pl.ds(row * CZ, CZ)] = high

time: 29.9 us -> 27.8 us (0.930)
  Pallas kernels: 28.5 us -> 26.4 us
    pallas_call x1, Pallas kernels: 26.8 us -> 24.3 us  [paint(): pl.pallas_call(functools.partial(paint_kernel, dims), out_shape=jax.Shape...]
    pallas_call x1, Pallas kernels: 1.66 us -> 2.01 us  [waves(): pl.pallas_call(functools.partial(wave_kernel, groups), out_shape=[jax.Sha...]
where the time goes in v3:
time: 27.8 us; the launch traced here: 27.7 us
  Pallas kernels  26.4 us (95%)
  between operations  1.3 us (5%)
    pallas_call x1, Pallas kernels, paint(): pl.pallas_call(functools.partial(paint_kernel, dims), out_shape=jax.Shape...  24.3 us
    pallas_call x1, Pallas kernels, waves(): pl.pallas_call(functools.partial(wave_kernel, groups), out_shape=[jax.Sha...  2.01 us

profile of v3, /device:TPU:0, one launch (start us, length us, event | category | flops | bytes accessed | tf_op | source)
XLA Modules:
  0.0 27.7 jit_solution(18369801773738178891)
XLA Ops:
  1.3 0.0 copy-start
  1.3 24.3 %shard_map.68.in_ref = f32[4,264,128]{2,1,0:T(8,128)S(1)} custom-call(s32[1]{0:T(128)} %bitcast.10.live_ref, s32[64,128]{1,0:T(8,128)} %bitcast.14, f32[3,64,128]{2,1,0:T(8,128)} %bitcast.13, f32[64,128]{1,0:T(8,128)} %bitcast.15), custom_call_target="tpu_custom_call" | custom-call | flops 10737418240 | bytes 196608 | tf_op jit(solution)/shard_map/pallas_call | solution.py:396
  25.6 0.0 copy-done
  25.6 2.0 %shard_map.69 = (f32[1024,128]{1,0:T(8,128)}, f32[1024,128]{1,0:T(8,128)}) custom-call(f32[4,264,128]{2,1,0:T(8,128)S(1)} %shard_map.68.in_ref, bf16[2,512,512]{2,1,0:T(8,128)(2,1)S(1)} %copy-done), custom_call_target="tpu_custom_call" | custom-call | tf_op jit(solution)/shard_map/pallas_call | solution.py:476
Async XLA Ops:
  1.3 24.4 %copy-start = (bf16[2,512,512]{2,1,0:T(8,128)(2,1)S(1)}, bf16[2,512,512]{2,1,0:T(8,128)(2,1)}, u32[]{:S(2)}) copy-start(bf16[2,512,512]{2,1,0:T(8,128)(2,1)} %constant.2.clone.table) | copy-start | bytes 3145732

commit v4 on v3

--- a/solution.py
+++ b/solution.py
@@ -42,7 +42,7 @@
     return high, value - high
 
 
-def paint_kernel(dims, live_ref, cell_hbm, off_hbm, mass_hbm, out_ref, cell_ref, off_ref, mass_ref, rows_x, rows_z, weigh, spot, zrhs, xrhs, lhs, glhs, crhs, fold_z, zin, yout, yin, pen, load, z_send, z_recv, y_send, y_recv, x_send, x_recv):
+def paint_kernel(dims, live_ref, cell_hbm, off_hbm, mass_hbm, out_ref, cell_ref, off_ref, mass_ref, rows_x, rows_z, weigh, spot, zrhs, xrhs, lhs, glhs, crhs, fold_z, zin, yout, yin, fout, fin, pen, load, z_send, z_recv, y_send, y_recv, f_send, f_recv, x_send, x_recv, opened):
     groups, count_y, count_z = dims
     padded_y = YP * groups + 2
     band = up(padded_y, 16)
@@ -67,7 +67,6 @@
         pl.semaphore_signal(barrier, inc=1, device_id={"gy": other}, device_id_type=MESH)
     for step in range(1, groups):
         pl.semaphore_signal(barrier, inc=1, device_id={"gx": lax.rem(gx + step, groups)}, device_id_type=MESH)
-
     for copy in loads:
         copy.wait()
     live = live_ref[0]
@@ -199,7 +198,7 @@
 
     y_copies = [
         pltpu.make_async_remote_copy(
-            src_ref=yout.at[pl.ds(side * CX, CX)],
+            src_ref=yout.at[side],
             dst_ref=yin.at[side],
             send_sem=y_send.at[side],
             recv_sem=y_recv.at[side],
@@ -207,41 +206,57 @@
             device_id_type=MESH,
         )
         for side in range(2)
-    ] + [
+    ]
+    far_copies = [
         pltpu.make_async_remote_copy(
-            src_ref=yout.at[pl.ds(BODY, 8)],
-            dst_ref=yin.at[2 + side, pl.ds(0, 8)],
-            send_sem=y_send.at[2 + side],
-            recv_sem=y_recv.at[2 + side],
-            device_id={"gy": y_next[side]},
+            src_ref=fout.at[side],
+            dst_ref=fin.at[gx],
+            send_sem=f_send.at[side],
+            recv_sem=f_recv.at[gx],
+            device_id={"gx": jnp.int32((groups - 1) * (1 - side)), "gy": y_next[side]},
             device_id_type=MESH,
         )
         for side in range(2)
     ]
-    def put(target, place, rows, at):
+
+    def put(target, main, edge, pitch, rows, at):
         edges = rows[YP]
-        target[pl.ds(pl.multiple_of(place * CX, 8), CX)] = rows[at]
+        target[pl.ds(main, CX)] = rows[at]
         for side in range(2):
             low = 4 * at + side
-            target[pl.ds(BODY + 2 * side + place, 1)] = edges[low : low + 1] + edges[low + 2 : low + 3]
-
-    def finish(target, place, index):
+            target[pl.ds(edge + pitch * side, 1)] = edges[low : low + 1] + edges[low + 2 : low + 3]
+
+    def put_pen(target, place, rows, at):
+        put(pen.at[target], pl.multiple_of(place * CX, 8), BODY + place, 2, rows, at)
+
+    def corners(index):
         ends = [zin[side, 1, pl.ds(index, 1)] for side in range(2)]
         for side in range(2):
             extra = jnp.where(edge_lane == CZ - 1, ends[0][:, side : side + 1], 0.0)
-            extra = extra + jnp.where(edge_lane == 0, ends[1][:, side : side + 1], 0.0)
-            target[pl.ds(BODY + 2 * side + place, 1)] += extra
-            target[pl.ds(BODY + 4 + 2 * side + place, 1)] = zin[side, 0, pl.ds(index, 1)]
+            yield extra + jnp.where(edge_lane == 0, ends[1][:, side : side + 1], 0.0)
+
+    def finish(target, place):
+        index = 1 + target * YP + place
+        for side, extra in enumerate(corners(index)):
+            pen[target, pl.ds(BODY + 2 * side + place, 1)] += extra
+            pen[target, pl.ds(BODY + 4 + 2 * side + place, 1)] = zin[side, 0, pl.ds(index, 1)]
+
+    def send_corners():
+        for side, index in enumerate((0, padded_y - 1)):
+            for kind, extra in enumerate(corners(index)):
+                fout[side, pl.ds(kind, 1)] = extra
+                fout[side, pl.ds(2 + kind, 1)] = zin[kind, 0, pl.ds(index, 1)]
+            far_copies[side].start()
 
     def add_first():
-        pen[0, pl.ds(0, CX)] += yin[1]
-        for kind in range(4):
-            pen[0, pl.ds(BODY + 2 * kind, 1)] += yin[3, pl.ds(2 * kind + 1, 1)]
+        pen[0, pl.ds(0, CX)] += yin[1, pl.ds(0, CX)]
+        for side in range(2):
+            pen[0, pl.ds(BODY + 2 * side, 1)] += yin[1, pl.ds(CX + side, 1)]
 
     def add_last():
-        pen[groups - 1, pl.ds((YP - 1) * CX, CX)] += yin[0]
-        for kind in range(4):
-            pen[groups - 1, pl.ds(BODY + 2 * kind + YP - 1, 1)] += yin[2, pl.ds(2 * kind, 1)]
+        pen[groups - 1, pl.ds((YP - 1) * CX, CX)] += yin[0, pl.ds(0, CX)]
+        for side in range(2):
+            pen[groups - 1, pl.ds(BODY + 2 * side + YP - 1, 1)] += yin[0, pl.ds(CX + side, 1)]
 
     late = groups - half
 
@@ -259,8 +274,16 @@
     leader = pencil_of(jnp.int32(0))
     rows = paint_rows(*as_float([line_of(leader, place) for place in range(YP)]))
     for place in range(YP):
-        put(pen.at[leader], place, rows, place)
+        put_pen(leader, place, rows, place)
     pl.semaphore_wait(barrier, groups + 3)
+
+    @pl.when(jnp.logical_or(gx == 0, gx == groups - 1))
+    def _():
+        for step in range(1, groups):
+            pl.semaphore_signal(
+                opened, inc=1, device_id={"gx": lax.rem(gx + step, groups)}, device_id_type=MESH
+            )
+
     for part in range(YP):
         part_copy(leader, part).start()
 
@@ -276,14 +299,15 @@
         for side in range(2)
     ]
     def send_ghosts():
-        step = pieces // 2
-        sums = []
+        step = span // 2
+        terms = ([], [])
         for piece in range(pieces):
             across(piece, build_x)
             across(piece, build_ghost)
-        for side in range(2):
-            starts = [piece * span for piece in range(side * step, step if side == 0 else pieces)]
-            sums.append(total(nt_dot(wide(glhs, start, span), wide(xrhs, start, span)) for start in starts))
+            for side in range(2):
+                start = piece * span + side * step
+                terms[side].append(nt_dot(wide(glhs, start, step), wide(xrhs, start, step)))
+        sums = [total(terms[side]) for side in range(2)]
         ends = total(nt_dot(wide(glhs, piece * span, span), wide(crhs, piece * span, span)) for piece in range(pieces))
         sums = gather(sums[0] + sums[1], 2 * band)
         ends = ends[: 2 * band] + ends[2 * band :]
@@ -296,80 +320,94 @@
         for copy in z_copies:
             copy.start()
 
-    pl.when(gx >= 0)(send_ghosts)
+    yout[:, pl.ds(CX, 8)] = jnp.zeros((2, 8, CZ), jnp.float32)
+    fout[...] = jnp.zeros_like(fout)
     held, close = pencil_of(jnp.int32(late - 1)), pencil_of(jnp.int32(late))
 
     def visit(turn, carry):
-        ghost = turn == 1
         whole = pencil_of(turn - 1)
-        early, second = turn == late, turn == late + 1
-        split_turn = jnp.logical_or(early, second)
-        targets = (jnp.where(split_turn, held, whole), jnp.where(split_turn, close, whole))
-        places = (
-            jnp.where(early, upper, jnp.where(second, 1 - upper, 0)),
-            jnp.where(early, 1 - upper, jnp.where(second, upper, 1)),
-        )
-        lines = [line_of(target, place) for target, place in zip(targets, places)]
-        lines = (jnp.where(ghost, 0, lines[0]), jnp.where(ghost, padded_y - 1, lines[1]))
-        rows = paint_rows(*as_float(lines))
-
-        @pl.when(ghost)
+        opening, closing, joining = turn == 1, turn == late, turn == late + 1
+        first = jnp.where(joining, line_of(held, 1 - upper), line_of(whole, 0))
+        second = jnp.where(joining, line_of(close, upper), line_of(whole, 1))
+        first = jnp.where(opening, upper * (padded_y - 1), jnp.where(closing, line_of(close, 1 - upper), first))
+        second = jnp.where(opening, line_of(held, upper), jnp.where(closing, (1 - upper) * (padded_y - 1), second))
+        rows = paint_rows(*as_float((first, second)))
+
+        @pl.when(opening)
+        def _():
+            put_pen(held, upper, rows, 1)
+            part_copy(held, upper).start()
+            put(yout.at[upper], 0, CX, 1, rows, 0)
+            for side in range(2):
+                pl.when(upper == side)(y_copies[side].start)
+
+        @pl.when(closing)
+        def _():
+            put_pen(close, 1 - upper, rows, 0)
+            part_copy(close, 1 - upper).start()
+            put(yout.at[1 - upper], 0, CX, 1, rows, 1)
+            for side in range(2):
+                pl.when(upper == 1 - side)(y_copies[side].start)
+            send_ghosts()
+
+        @pl.when(joining)
+        def _():
+            put_pen(held, 1 - upper, rows, 0)
+            put_pen(close, upper, rows, 1)
+            for side in range(2):
+
+                @pl.when(upper == side)
+                def _():
+                    y_copies[side].wait()
+                    (add_first if side else add_last)()
+
+            part_copy(held, 1 - upper).start()
+            for copy in z_copies:
+                copy.wait()
+            pl.semaphore_wait(opened, jnp.where(jnp.logical_or(gx == 0, gx == groups - 1), 1, 2))
+            send_corners()
+            for order in range(late):
+                target = pencil_of(jnp.int32(order))
+                for place in range(YP):
+                    finish(target, place)
+                part_copy(target, YP).start()
+            for place in range(YP):
+                finish(close, place)
+            for side in range(2):
+
+                @pl.when(upper == 1 - side)
+                def _():
+                    y_copies[side].wait()
+                    pl.when(gx != (groups - 1) * (1 - side))(add_first if side else add_last)
+
+            part_copy(close, upper).start()
+            part_copy(close, YP).start()
+
+        @pl.when(jnp.logical_not(jnp.logical_or(opening, jnp.logical_or(closing, joining))))
         def _():
             for place in range(YP):
-                put(yout, place, rows, place)
-            for copy in z_copies:
-                copy.wait()
-            for place, line in enumerate(lines):
-                finish(yout, place, line)
-            for copy in y_copies:
-                copy.start()
-            for place in range(YP):
-                finish(pen.at[leader], place, line_of(leader, place))
-            part_copy(leader, YP).start()
-
-        @pl.when(jnp.logical_not(ghost))
-        def _():
-            for at, (target, place) in enumerate(zip(targets, places)):
-                put(pen.at[target], place, rows, at)
-
-            @pl.when(early)
+                put_pen(whole, place, rows, place)
+
+            @pl.when(turn < late)
             def _():
-                for target, place in zip(targets, places):
-                    part_copy(target, place).start()
-
-            for target, place, line in zip(targets, places, lines):
-                finish(pen.at[target], place, line)
-
-            @pl.when(second)
+                for place in range(YP):
+                    part_copy(whole, place).start()
+
+            @pl.when(turn > late + 1)
             def _():
-                for copy in y_copies:
-                    copy.wait()
-
-            @pl.when(jnp.logical_or(jnp.logical_and(second, gx != 0), jnp.logical_and(turn == groups, gx == 0)))
-            def _():
-                add_first()
-
-            @pl.when(
-                jnp.logical_or(
-                    jnp.logical_and(second, gx != groups - 1), jnp.logical_and(turn == groups, gx == groups - 1)
-                )
-            )
-            def _():
-                add_last()
-
-            @pl.when(jnp.logical_and(turn < groups, jnp.logical_not(early)))
-            def _():
-                for target, place in zip(targets, places):
-                    part_copy(target, place).start()
-                part_copy(targets[0], YP).start()
-
-            @pl.when(second)
-            def _():
-                part_copy(close, YP).start()
+                for place in range(YP):
+                    finish(whole, place)
+
+                @pl.when(turn < groups)
+                def _():
+                    for part in range(YP + 1):
+                        part_copy(whole, part).start()
 
         return carry
 
     lax.fori_loop(1, groups + 1, visit, 0)
+    pl.when(gx == 0)(add_first)
+    pl.when(gx == groups - 1)(add_last)
     out_ref[gx] = pen[gx]
     for step in range(1, groups):
         source = lax.rem(gx + step, groups)
@@ -384,6 +422,24 @@
                 device_id={"gx": source},
                 device_id_type=MESH,
             ).wait_recv()
+    for side in range(2):
+        far_copies[side].wait_send()
+    for side, owner in enumerate((groups - 1, 0)):
+
+        @pl.when(gx == owner)
+        def _():
+            for source in range(groups):
+                pltpu.make_async_remote_copy(
+                    src_ref=fout.at[side],
+                    dst_ref=fin.at[source],
+                    send_sem=f_send.at[side],
+                    recv_sem=f_recv.at[source],
+                    device_id={"gx": jnp.int32(source), "gy": y_next[side]},
+                    device_id_type=MESH,
+                ).wait_recv()
+                for kind in range(4):
+                    at = pl.ds(BODY + 2 * kind + (YP - 1) * (1 - side), 1)
+                    out_ref[source, at] += fin[source, pl.ds(kind, 1)]
 
 
 def paint(dims, cell, offs, mass, live):
@@ -413,16 +469,21 @@
             pltpu.VMEM((lines, 16, 128), jnp.bfloat16),
             pltpu.VMEM((2, 2, band, CX), jnp.float32),
             pltpu.VMEM((2, 2, band, CX), jnp.float32),
-            pltpu.VMEM((ROWS, CZ), jnp.float32),
-            pltpu.VMEM((4, CX, CZ), jnp.float32),
+            pltpu.VMEM((2, CX + 8, CZ), jnp.float32),
+            pltpu.VMEM((2, CX + 8, CZ), jnp.float32),
+            pltpu.VMEM((2, 8, CZ), jnp.float32),
+            pltpu.VMEM((groups, 8, CZ), jnp.float32),
             pltpu.VMEM((groups, ROWS, CZ), jnp.float32),
             dma((3,)),
             dma((2,)),
             dma((2,)),
-            dma((4,)),
-            dma((4,)),
+            dma((2,)),
+            dma((2,)),
+            dma((2,)),
+            dma((groups,)),
             dma((YP + 1, groups)),
             dma((YP + 1, groups)),
+            pltpu.SemaphoreType.REGULAR,
         ],
         cost_estimate=pl.CostEstimate(flops=work, bytes_accessed=24 * lines * 128, transcendentals=0),
         compiler_params=pltpu.CompilerParams(
@@ -431,11 +492,12 @@
     )(live, *(pltpu.with_memory_space_constraint(value, pltpu.HBM) for value in (cell, offs, mass)))
 
 
-def wave_kernel(groups, in_ref, table, dens_ref, spec_ref, flat):
+def wave_kernel(groups, in_ref, table, dens_hbm, spec_hbm, flat, dens_ref, spec_ref, sems):
     length = groups * CX
     row_id = lax.broadcasted_iota(jnp.int32, (CX, CZ), 0)
     lane = lax.broadcasted_iota(jnp.int32, (CX, CZ), 1)
     columns = jnp.concatenate([in_ref[block, BODY:ROWS] for block in range(groups)], axis=0).T
+    copies = []
     for block in range(groups):
         before, after = (block - 1) % groups, (block + 1) % groups
         for row in range(YP):
@@ -450,19 +512,23 @@
             high, low = split(value)
             flat[0, pl.ds(block * CX, CX), pl.ds(row * CZ, CZ)] = high
             flat[1, pl.ds(block * CX, CX), pl.ds(row * CZ, CZ)] = low
-    tile = 256
-
-    def transform(turn, carry):
-        start = pl.multiple_of(turn * tile, tile)
-        rows = pl.ds(start, tile)
+        here = pl.ds(block * BODY, BODY)
+        copies.append(pltpu.make_async_copy(dens_ref.at[here], dens_hbm.at[here], sems.at[block]))
+        copies[-1].start()
+    tiles = 4
+    tile = length // tiles
+    for turn in range(tiles):
+        rows = pl.ds(turn * tile, tile)
         both = jnp.dot(table[0, rows, :], flat[0], preferred_element_type=jnp.float32)
         both += jnp.dot(table[1, rows, :], flat[0], preferred_element_type=jnp.float32)
         both += jnp.dot(table[0, rows, :], flat[1], preferred_element_type=jnp.float32)
         for row in range(YP):
-            spec_ref[pl.ds(start * YP + row, tile, stride=YP), :] = both[:, row * CZ : (row + 1) * CZ]
-        return carry
-
-    lax.fori_loop(0, length // tile, transform, 0)
+            spec_ref[pl.ds(turn * tile * YP + row, tile, stride=YP), :] = both[:, row * CZ : (row + 1) * CZ]
+        here = pl.ds(turn * tile * YP, tile * YP)
+        copies.append(pltpu.make_async_copy(spec_ref.at[here], spec_hbm.at[here], sems.at[groups + turn]))
+        copies[-1].start()
+    for copy in copies:
+        copy.wait()
 
 
 def waves(groups, pencils):
@@ -480,8 +546,13 @@
             jax.ShapeDtypeStruct((2 * half * YP, CZ), jnp.float32),
         ],
         in_specs=[vmem] * 2,
-        out_specs=[vmem] * 2,
-        scratch_shapes=[pltpu.VMEM((2, length, YP * CZ), jnp.bfloat16)],
+        out_specs=[pl.BlockSpec(memory_space=pltpu.HBM)] * 2,
+        scratch_shapes=[
+            pltpu.VMEM((2, length, YP * CZ), jnp.bfloat16),
+            pltpu.VMEM((length * YP, CZ), jnp.float32),
+            pltpu.VMEM((2 * half * YP, CZ), jnp.float32),
+            pltpu.SemaphoreType.DMA((groups + 4,)),
+        ],
         compiler_params=pltpu.CompilerParams(vmem_limit_bytes=24 * 1024 * 1024),
     )(pencils, jnp.asarray(np.stack([fhi, flo])))
 

time: 27.8 us -> 27.5 us (0.989)
  Pallas kernels: 26.4 us -> 26.1 us
where the time goes in v4:
time: 27.5 us; the launch traced here: 27.4 us
  Pallas kernels  26.1 us (95%)
  between operations  1.3 us (5%)
    pallas_call x1, Pallas kernels, paint(): pl.pallas_call(functools.partial(paint_kernel, dims), out_shape=jax.Shape...  24.1 us
    pallas_call x1, Pallas kernels, waves(): pl.pallas_call(functools.partial(wave_kernel, groups), out_shape=[jax.Sha...  1.94 us

profile of v4, /device:TPU:0, one launch (start us, length us, event | category | flops | bytes accessed | tf_op | source)
XLA Modules:
  0.0 27.4 jit_solution(17129456937381780545)
XLA Ops:
  1.3 0.0 copy-start
  1.3 24.1 %shard_map.68.in_ref = f32[4,264,128]{2,1,0:T(8,128)S(1)} custom-call(s32[1]{0:T(128)} %bitcast.10.live_ref, s32[64,128]{1,0:T(8,128)} %bitcast.14, f32[3,64,128]{2,1,0:T(8,128)} %bitcast.13, f32[64,128]{1,0:T(8,128)} %bitcast.15), custom_call_target="tpu_custom_call" | custom-call | flops 10737418240 | bytes 196608 | tf_op jit(solution)/shard_map/pallas_call | solution.py:452
  25.4 0.0 copy-done
  25.4 1.9 %shard_map.69 = (f32[1024,128]{1,0:T(8,128)}, f32[1024,128]{1,0:T(8,128)}) custom-call(f32[4,264,128]{2,1,0:T(8,128)S(1)} %shard_map.68.in_ref, bf16[2,512,512]{2,1,0:T(8,128)(2,1)S(1)} %copy-done), custom_call_target="tpu_custom_call" | custom-call | tf_op jit(solution)/shard_map/pallas_call | solution.py:542
Async XLA Ops:
  1.3 24.2 %copy-start = (bf16[2,512,512]{2,1,0:T(8,128)(2,1)S(1)}, bf16[2,512,512]{2,1,0:T(8,128)(2,1)}, u32[]{:S(2)}) copy-start(bf16[2,512,512]{2,1,0:T(8,128)(2,1)} %constant.2.clone.table) | copy-start | bytes 3145732

commit v5 on v4

--- a/solution.py
+++ b/solution.py
@@ -335,11 +335,11 @@
 
         @pl.when(opening)
         def _():
-            put_pen(held, upper, rows, 1)
-            part_copy(held, upper).start()
             put(yout.at[upper], 0, CX, 1, rows, 0)
             for side in range(2):
                 pl.when(upper == side)(y_copies[side].start)
+            put_pen(held, upper, rows, 1)
+            part_copy(held, upper).start()
 
         @pl.when(closing)
         def _():
@@ -353,7 +353,6 @@
         @pl.when(joining)
         def _():
             put_pen(held, 1 - upper, rows, 0)
-            put_pen(close, upper, rows, 1)
             for side in range(2):
 
                 @pl.when(upper == side)
@@ -362,6 +361,7 @@
                     (add_first if side else add_last)()
 
             part_copy(held, 1 - upper).start()
+            put_pen(close, upper, rows, 1)
             for copy in z_copies:
                 copy.wait()
             pl.semaphore_wait(opened, jnp.where(jnp.logical_or(gx == 0, gx == groups - 1), 1, 2))

time: 27.5 us -> 27.5 us (level)
  no operation moved by 1% of the time
where the time goes in v5:
time: 27.5 us; the launch traced here: 27.4 us
  Pallas kernels  26.1 us (95%)
  between operations  1.3 us (5%)
    pallas_call x1, Pallas kernels, paint(): pl.pallas_call(functools.partial(paint_kernel, dims), out_shape=jax.Shape...  24.1 us
    pallas_call x1, Pallas kernels, waves(): pl.pallas_call(functools.partial(wave_kernel, groups), out_shape=[jax.Sha...  1.94 us

profile of v5, /device:TPU:0, one launch (start us, length us, event | category | flops | bytes accessed | tf_op | source)
XLA Modules:
  0.0 27.4 jit_solution(4585006305518361515)
XLA Ops:
  1.3 0.0 copy-start
  1.3 24.1 %shard_map.68.in_ref = f32[4,264,128]{2,1,0:T(8,128)S(1)} custom-call(s32[1]{0:T(128)} %bitcast.10.live_ref, s32[64,128]{1,0:T(8,128)} %bitcast.14, f32[3,64,128]{2,1,0:T(8,128)} %bitcast.13, f32[64,128]{1,0:T(8,128)} %bitcast.15), custom_call_target="tpu_custom_call" | custom-call | flops 10737418240 | bytes 196608 | tf_op jit(solution)/shard_map/pallas_call | solution.py:452
  25.4 0.0 copy-done
  25.4 1.9 %shard_map.69 = (f32[1024,128]{1,0:T(8,128)}, f32[1024,128]{1,0:T(8,128)}) custom-call(f32[4,264,128]{2,1,0:T(8,128)S(1)} %shard_map.68.in_ref, bf16[2,512,512]{2,1,0:T(8,128)(2,1)S(1)} %copy-done), custom_call_target="tpu_custom_call" | custom-call | tf_op jit(solution)/shard_map/pallas_call | solution.py:542
Async XLA Ops:
  1.3 24.1 %copy-start = (bf16[2,512,512]{2,1,0:T(8,128)(2,1)S(1)}, bf16[2,512,512]{2,1,0:T(8,128)(2,1)}, u32[]{:S(2)}) copy-start(bf16[2,512,512]{2,1,0:T(8,128)(2,1)} %constant.2.clone.table) | copy-start | bytes 3145732
